TPU v7x, 32 devices: a whole 2x2x4 slice. The times are simulated.
32 devices in a mesh: gx: 8 (over y, x, core), gy: 4 (over z).
Axes of the slice: x: 2, y: 2, z: 4, core: 2. Of those that a mesh axis runs over, the one named last changes fastest.
Arguments:
- right_side: float32 [1024, 2048], P('gx', 'gy'), may hold values from -6 to 6
- kappa_field: float32 [1024, 2048], P('gx', 'gy'), may hold values from 0.0001 to 0.01
- ice_blocks: int32 [128, 256], P('gx', 'gy'), may hold values 0 or 1
Outputs:
- solution_field: float32 [1024, 2048], P('gx', 'gy')
All inputs are finite; a program needn't handle non-finite values. No bound on the sum of `ice_blocks` on one device may be relied on, other than what follows from the above.
Results may differ from a plain program's by a relative error of at most 0.0001.
Values sent between devices are 32-bit elements; how exact they have to be, the bound alone decides.
No kernel may reach another device: no remote copies, remote signals or barrier semaphores. Data moves between devices by JAX's collectives and lax.ppermute only.
A program may use at most 64 MiB of HBM per device.

v0:
```python
import jax
import jax.numpy as jnp
from jax import lax
from jax.sharding import PartitionSpec as P

BLOCK = 8
NC = 16


damping = 0.8


def with_halo(cells, sides, width):
    for axis, dim in sides:
        count = lax.axis_size(axis)
        ends = count - 1
        head = lax.slice_in_dim(cells, 0, width, axis=dim)
        tail = lax.slice_in_dim(cells, cells.shape[dim] - width, cells.shape[dim], axis=dim)
        cells = jnp.concatenate(
            [
                lax.ppermute(tail, axis, [(i, (i + 1) % count) for i in range(ends)]),
                cells,
                lax.ppermute(head, axis, [((i + 1) % count, i) for i in range(ends)]),
            ],
            axis=dim,
        )
    return cells


def apply_operator(padded, reaction, stiffness):
    middle = padded[1:-1, 1:-1]
    beside = padded[2:, 1:-1] + padded[:-2, 1:-1]
    beside = beside + padded[1:-1, 2:] + padded[1:-1, :-2]
    return reaction * middle + stiffness * (4.0 * middle - beside)


def jacobi_step(padded, source, reaction, stiffness):
    middle = padded[1:-1, 1:-1]
    applied = apply_operator(padded, reaction, stiffness)
    return middle + damping * (source - applied) / (reaction + 4.0 * stiffness)


def restrict(field):
    height, width = field.shape
    return field.reshape(height // 2, 2, width // 2, 2).mean(axis=(1, 3))


def prolong(field):
    return jnp.repeat(jnp.repeat(field, 2, axis=0), 2, axis=1)


def extend(field, margin):
    return with_halo(field, (("gx", 0), ("gy", 1)), margin)


def level_margins(source, reaction):
    stacked = jnp.stack((source, reaction), axis=0)
    widened = with_halo(stacked, (("gx", 1), ("gy", 2)), 1)
    return (widened[0], widened[1])


def inside_region(height, width, margin):
    row_index = (
        lax.axis_index("gx") * height + jnp.arange(height + 2 * margin, dtype=jnp.int32) - margin
    )
    col_index = (
        lax.axis_index("gy") * width + jnp.arange(width + 2 * margin, dtype=jnp.int32) - margin
    )
    row_valid = (row_index >= 0) & (row_index < height * lax.axis_size("gx"))
    col_valid = (col_index >= 0) & (col_index < width * lax.axis_size("gy"))
    return (row_valid[:, None] & col_valid[None, :]).astype(jnp.float32)


def deep_sweeps(field, source, reaction, source_rim, reaction_rim, stiffness):
    height, width = field.shape
    keeper = inside_region(height, width, 1)
    wider = extend(field, 2)
    middle = jacobi_step(wider, source_rim, reaction_rim, stiffness) * keeper
    field = jacobi_step(middle, source, reaction, stiffness)
    return field


def smooth(field, source, reaction, stiffness, margins):
    field = deep_sweeps(field, source, reaction, margins[0], margins[1], stiffness)
    return field


def per_device(right_side, kappa_field, ice_blocks):
    ice = jnp.repeat(jnp.repeat(ice_blocks, BLOCK, axis=0), BLOCK, axis=1).astype(jnp.float32)
    reaction = kappa_field * (1.0 + 3.0 * (1.0 - ice))
    source = right_side
    stored = []
    for level in range(3):
        stiffness = 0.25**level
        margins = level_margins(source, reaction)
        field = smooth(jnp.zeros_like(source), source, reaction, stiffness, margins)
        stored.append((field, source, reaction, margins))
        residual = source - apply_operator(extend(field, 1), reaction, stiffness)
        source = restrict(residual)
        reaction = restrict(reaction)
    height, width = source.shape
    stacked = jnp.stack((source, reaction), axis=0)
    region = with_halo(stacked, (("gx", 1), ("gy", 2)), NC)
    region_source = region[0]
    region_reaction = region[1]
    keeper = inside_region(height, width, NC)
    coarse = jnp.zeros_like(region_source)
    for sweep in range(NC):
        coarse = jacobi_step(jnp.pad(coarse, 1), region_source, region_reaction, 0.25**3) * keeper
    field = coarse[NC : NC + height, NC : NC + width]
    for level in (2, 1, 0):
        stiffness = 0.25**level
        before, source, reaction, margins = stored[level]
        field = smooth(before + prolong(field), source, reaction, stiffness, margins)
    return field


def solution(mesh):
    in_specs = (P("gx", "gy"), P("gx", "gy"), P("gx", "gy"))
    out_specs = P("gx", "gy")
    return jax.shard_map(
        per_device, mesh=mesh, in_specs=in_specs, out_specs=out_specs, check_vma=False
    )
```

profile of v0, /device:TPU:3, one launch (start us, length us, event | category | flops | bytes accessed | tf_op | source)
XLA Modules:
  0.0 287.8 jit_solution(4702534781917893370)
XLA Ops:
  0.0 3.8 %collective-permute-start = (f32[2,512]{0,1:T(8,128)S(1)}, f32[2,512]{0,1:T(8,128)S(1)}, u32[]{:S(2)}, u32[]{:S(2)}) collective-permute-start(f32[2,512]{0,1:T(8,128)S(1)} %broadcast.431), channel_id=1, source_target_pairs={{0,4},{4,8},{8,12},{12,16},{16,20},{20,24},{24,28},{1,5},{5,9},{9,... | collective-permute-start | bytes 12296 | tf_op jit(solution)/shard_map/ppermute | solution.py:21
  8.8 4.5 %collective-permute-start.4 = (f32[2,1,512]{1,2,0:T(8,128)}, f32[2,1,512]{1,2,0:T(8,128)S(1)}, u32[]{:S(2)}, u32[]{:S(2)}) collective-permute-start(f32[2,1,512]{1,2,0:T(8,128)} %get-tuple-element.15), channel_id=1, source_target_pairs={{0,4},{4,8},{8,12},{12,16},{16,20},{20,24},{24,28},{1,5},{5,9},{9,... | collective-permute-start | bytes 12296 | tf_op jit(solution)/shard_map/ppermute | solution.py:21
  15.3 4.5 %collective-permute-start.8 = (f32[2,256]{1,0:T(2,128)S(1)}, f32[2,256]{1,0:T(2,128)S(1)}, u32[]{:S(2)}, u32[]{:S(2)}) collective-permute-start(f32[2,256]{1,0:T(2,128)S(1)} %broadcast.445), channel_id=1, source_target_pairs={{0,4},{4,8},{8,12},{12,16},{16,20},{20,24},{24,28},{1,5},{5,9},{9,... | collective-permute-start | bytes 6152 | tf_op jit(solution)/shard_map/ppermute | solution.py:21
  20.0 18.1 %reshape.171 = f32[64,2,256,2]{3,2,1,0:T(8,128)} reshape(f32[128,512]{1,0:T(8,128)S(1)} %copy.61) | data formatting | bytes 524288 | tf_op jit(solution)/shard_map/reshape | solution.py:45
  38.1 8.0 %reduce_sum.55 = f32[64,256]{1,0:T(8,128)S(1)} reduce(f32[64,2,256,2]{3,2,1,0:T(8,128)} %reshape.171, f32[]{:T(128)} %constant.50.clone.1), dimensions={1,3}, to_apply=%region_1.0 | reduce | flops 49152 | bytes 327684 | tf_op jit(solution)/shard_map/reduce_sum | solution.py:45
  48.1 4.5 %collective-permute-start.20 = (f32[2,128]{1,0:T(2,128)S(1)}, f32[2,128]{1,0:T(2,128)S(1)}, u32[]{:S(2)}, u32[]{:S(2)}) collective-permute-start(f32[2,128]{1,0:T(2,128)S(1)} %broadcast.459), channel_id=1, source_target_pairs={{0,4},{4,8},{8,12},{12,16},{16,20},{20,24},{24,28},{1,5},{5,9},{9,... | collective-permute-start | bytes 3080 | tf_op jit(solution)/shard_map/ppermute | solution.py:21
  57.4 4.0 %collective-permute-start.2 = (f32[132,2]{0,1:T(2,128)S(1)}, f32[132,2]{0,1:T(2,128)S(1)}, u32[]{:S(2)}, u32[]{:S(2)}) collective-permute-start(f32[132,2]{0,1:T(2,128)S(1)} %get-tuple-element.14), channel_id=1, source_target_pairs={{0,1},{1,2},{2,3},{4,5},{5,6},{6,7},{8,9},{9,10},{10,11},{12,13},{... | collective-permute-start | bytes 3176 | tf_op jit(solution)/shard_map/ppermute | solution.py:21
  69.4 4.5 %collective-permute-start.13 = (f32[1,512]{0,1:T(8,128)S(1)}, f32[1,512]{0,1:T(8,128)S(1)}, u32[]{:S(2)}, u32[]{:S(2)}) collective-permute-start(f32[1,512]{0,1:T(8,128)S(1)} %get-tuple-element.19), channel_id=1, source_target_pairs={{0,4},{4,8},{8,12},{12,16},{16,20},{20,24},{24,28},{1,5},{5,9},{9,... | collective-permute-start | bytes 6152 | tf_op jit(solution)/shard_map/ppermute | solution.py:21
  74.0 3.8 %collective-permute-done.12 = f32[1,512]{0,1:T(8,128)S(1)} collective-permute-done((f32[1,512]{0,1:T(8,128)S(1)}, f32[1,512]{0,1:T(8,128)S(1)}, u32[]{:S(2)}, u32[]{:S(2)}) %collective-permute-start.12) | collective-permute-done | bytes 2080 | tf_op jit(solution)/shard_map/ppermute | solution.py:23
  81.1 4.0 %collective-permute-start.15 = (f32[130,1]{0,1:T(1,128)S(1)}, f32[130,1]{0,1:T(1,128)S(1)}, u32[]{:S(2)}, u32[]{:S(2)}) collective-permute-start(f32[130,1]{0,1:T(1,128)S(1)} %get-tuple-element.12), channel_id=1, source_target_pairs={{0,1},{1,2},{2,3},{4,5},{5,6},{6,7},{8,9},{9,10},{10,11},{12,13},{... | collective-permute-start | bytes 1568 | tf_op jit(solution)/shard_map/ppermute | solution.py:21
  86.3 18.1 %reshape.170 = f32[64,2,256,2]{3,2,1,0:T(8,128)} reshape(f32[128,512]{1,0:T(8,128)S(1)} %copy.60) | data formatting | bytes 524288 | tf_op jit(solution)/shard_map/reshape | solution.py:45
  104.4 8.0 %reduce_sum.54 = f32[64,256]{1,0:T(8,128)S(1)} reduce(f32[64,2,256,2]{3,2,1,0:T(8,128)} %reshape.170, f32[]{:T(128)} %constant.50.clone.1), dimensions={1,3}, to_apply=%region_0.0 | reduce | flops 49152 | bytes 327684 | tf_op jit(solution)/shard_map/reduce_sum | solution.py:45
  112.5 5.7 %collective-permute-start.16 = (f32[2,1,256]{2,1,0:T(1,128)S(1)}, f32[2,1,256]{2,1,0:T(1,128)S(1)}, u32[]{:S(2)}, u32[]{:S(2)}) collective-permute-start(f32[2,1,256]{2,1,0:T(1,128)S(1)} %get-tuple-element.23), channel_id=1, source_target_pairs={{0,4},{4,8},{8,12},{12,16},{16,20},{20,24},{24,28},{1,5},{5,9},{9,... | collective-permute-start | bytes 6152 | tf_op jit(solution)/shard_map/ppermute | solution.py:21
  120.1 3.9 %collective-permute-start.10 = (f32[68,2]{1,0:T(8,128)S(1)}, f32[68,2]{1,0:T(8,128)S(1)}, u32[]{:S(2)}, u32[]{:S(2)}) collective-permute-start(f32[68,2]{1,0:T(8,128)S(1)} %get-tuple-element.30), channel_id=1, source_target_pairs={{0,1},{1,2},{2,3},{4,5},{5,6},{6,7},{8,9},{9,10},{10,11},{12,13},{... | collective-permute-start | bytes 1640 | tf_op jit(solution)/shard_map/ppermute | solution.py:21
  125.5 4.0 %collective-permute-start.18 = (f32[2,66,1]{2,1,0:T(8,128)S(1)}, f32[2,66,1]{2,1,0:T(8,128)S(1)}, u32[]{:S(2)}, u32[]{:S(2)}) collective-permute-start(f32[2,66,1]{2,1,0:T(8,128)S(1)} %get-tuple-element.21), channel_id=1, source_target_pairs={{0,1},{1,2},{2,3},{4,5},{5,6},{6,7},{8,9},{9,10},{10,11},{12,13},{... | collective-permute-start | bytes 1592 | tf_op jit(solution)/shard_map/ppermute | solution.py:21
  131.1 3.7 %collective-permute-done.19 = f32[2,66,1]{2,1,0:T(8,128)S(1)} collective-permute-done((f32[2,66,1]{2,1,0:T(8,128)S(1)}, f32[2,66,1]{2,1,0:T(8,128)S(1)}, u32[]{:S(2)}, u32[]{:S(2)}) %collective-permute-start.19) | collective-permute-done | bytes 560 | tf_op jit(solution)/shard_map/ppermute | solution.py:23
  137.2 6.5 %collective-permute-start.25 = (f32[1,256]{1,0:T(1,128)S(1)}, f32[1,256]{1,0:T(1,128)S(1)}, u32[]{:S(2)}, u32[]{:S(2)}) collective-permute-start(f32[1,256]{1,0:T(1,128)S(1)} %get-tuple-element.35), channel_id=1, source_target_pairs={{0,4},{4,8},{8,12},{12,16},{16,20},{20,24},{24,28},{1,5},{5,9},{9,... | collective-permute-start | bytes 3080 | tf_op jit(solution)/shard_map/ppermute | solution.py:21
  145.9 4.0 %collective-permute-start.27 = (f32[66,1]{1,0:T(8,128)S(1)}, f32[66,1]{1,0:T(8,128)S(1)}, u32[]{:S(2)}, u32[]{:S(2)}) collective-permute-start(f32[66,1]{1,0:T(8,128)S(1)} %get-tuple-element.28), channel_id=1, source_target_pairs={{0,1},{1,2},{2,3},{4,5},{5,6},{6,7},{8,9},{9,10},{10,11},{12,13},{... | collective-permute-start | bytes 800 | tf_op jit(solution)/shard_map/ppermute | solution.py:21
  151.0 5.6 %reshape.172 = f32[32,2,128,2]{3,2,1,0:T(8,128)} reshape(f32[64,256]{1,0:T(8,128)S(1)} %get-tuple-element.33) | data formatting | bytes 131072 | tf_op jit(solution)/shard_map/reshape | solution.py:45
  159.4 5.6 %div.128 = f32[32,2,128,2]{3,2,1,0:T(8,128)} reshape(f32[64,256]{1,0:T(8,128)S(1)} %get-tuple-element.34) | data formatting | bytes 131072 | tf_op jit(solution)/shard_map/div | solution.py:45
  167.8 6.2 %collective-permute-start.28 = (f32[2,1,128]{2,1,0:T(1,128)S(1)}, f32[2,1,128]{2,1,0:T(1,128)S(1)}, u32[]{:S(2)}, u32[]{:S(2)}) collective-permute-start(f32[2,1,128]{2,1,0:T(1,128)S(1)} %get-tuple-element.43), channel_id=1, source_target_pairs={{0,4},{4,8},{8,12},{12,16},{16,20},{20,24},{24,28},{1,5},{5,9},{9,... | collective-permute-start | bytes 3080 | tf_op jit(solution)/shard_map/ppermute | solution.py:21
  176.0 3.9 %collective-permute-start.22 = (f32[36,2]{1,0:T(8,128)S(1)}, f32[36,2]{1,0:T(8,128)S(1)}, u32[]{:S(2)}, u32[]{:S(2)}) collective-permute-start(f32[36,2]{1,0:T(8,128)S(1)} %get-tuple-element.50), channel_id=1, source_target_pairs={{0,1},{1,2},{2,3},{4,5},{5,6},{6,7},{8,9},{9,10},{10,11},{12,13},{... | collective-permute-start | bytes 872 | tf_op jit(solution)/shard_map/ppermute | solution.py:21
  181.4 4.0 %collective-permute-start.30 = (f32[2,34,1]{2,1,0:T(8,128)S(1)}, f32[2,34,1]{2,1,0:T(8,128)S(1)}, u32[]{:S(2)}, u32[]{:S(2)}) collective-permute-start(f32[2,34,1]{2,1,0:T(8,128)S(1)} %get-tuple-element.41), channel_id=1, source_target_pairs={{0,1},{1,2},{2,3},{4,5},{5,6},{6,7},{8,9},{9,10},{10,11},{12,13},{... | collective-permute-start | bytes 824 | tf_op jit(solution)/shard_map/ppermute | solution.py:21
  192.4 6.5 %collective-permute-start.33 = (f32[1,128]{1,0:T(1,128)S(1)}, f32[1,128]{1,0:T(1,128)S(1)}, u32[]{:S(2)}, u32[]{:S(2)}) collective-permute-start(f32[1,128]{1,0:T(1,128)S(1)} %get-tuple-element.55), channel_id=1, source_target_pairs={{0,4},{4,8},{8,12},{12,16},{16,20},{20,24},{24,28},{1,5},{5,9},{9,... | collective-permute-start | bytes 1544 | tf_op jit(solution)/shard_map/ppermute | solution.py:21
  201.1 4.0 %collective-permute-start.35 = (f32[34,1]{1,0:T(8,128)S(1)}, f32[34,1]{1,0:T(8,128)S(1)}, u32[]{:S(2)}, u32[]{:S(2)}) collective-permute-start(f32[34,1]{1,0:T(8,128)S(1)} %get-tuple-element.48), channel_id=1, source_target_pairs={{0,1},{1,2},{2,3},{4,5},{5,6},{6,7},{8,9},{9,10},{10,11},{12,13},{... | collective-permute-start | bytes 416 | tf_op jit(solution)/shard_map/ppermute | solution.py:21
  208.5 6.2 %collective-permute-start.36 = (f32[2,16,64]{2,1,0:T(8,128)S(1)}, f32[2,16,64]{2,1,0:T(8,128)S(1)}, u32[]{:S(2)}, u32[]{:S(2)}) collective-permute-start(f32[2,16,64]{2,1,0:T(8,128)S(1)} %pad_maximum_fusion.80), channel_id=1, source_target_pairs={{0,4},{4,8},{8,12},{12,16},{16,20},{20,24},{24,28},{1,5},{5,9},{9,... | collective-permute-start | bytes 24584 | tf_op jit(solution)/shard_map/ppermute | solution.py:21
  216.7 4.0 %collective-permute-done.37 = f32[2,16,64]{2,1,0:T(8,128)S(1)} collective-permute-done((f32[2,16,64]{2,1,0:T(8,128)S(1)}, f32[2,16,64]{2,1,0:T(8,128)S(1)}, u32[]{:S(2)}, u32[]{:S(2)}) %collective-permute-start.37) | collective-permute-done | bytes 8224 | tf_op jit(solution)/shard_map/ppermute | solution.py:23
  220.8 3.9 %collective-permute-start.38 = (f32[2,48,16]{2,1,0:T(8,128)S(1)}, f32[2,48,16]{2,1,0:T(8,128)S(1)}, u32[]{:S(2)}, u32[]{:S(2)}) collective-permute-start(f32[2,48,16]{2,1,0:T(8,128)S(1)} %get-tuple-element.39), channel_id=1, source_target_pairs={{0,1},{1,2},{2,3},{4,5},{5,6},{6,7},{8,9},{9,10},{10,11},{12,13},{... | collective-permute-start | bytes 18440 | tf_op jit(solution)/shard_map/ppermute | solution.py:21
  226.1 3.5 %collective-permute-done.39 = f32[2,48,16]{2,1,0:T(8,128)S(1)} collective-permute-done((f32[2,48,16]{2,1,0:T(8,128)S(1)}, f32[2,48,16]{2,1,0:T(8,128)S(1)}, u32[]{:S(2)}, u32[]{:S(2)}) %collective-permute-start.39) | collective-permute-done | bytes 6176 | tf_op jit(solution)/shard_map/ppermute | solution.py:23
  236.8 3.9 %collective-permute-done.41 = f32[2,128]{1,0:T(2,128)S(1)} collective-permute-done((f32[2,128]{1,0:T(2,128)S(1)}, f32[2,128]{1,0:T(2,128)S(1)}, u32[]{:S(2)}, u32[]{:S(2)}) %collective-permute-start.41) | collective-permute-done | bytes 1056 | tf_op jit(solution)/shard_map/ppermute | solution.py:23
  254.5 3.9 %collective-permute-done.45 = f32[2,256]{1,0:T(2,128)S(1)} collective-permute-done((f32[2,256]{1,0:T(2,128)S(1)}, f32[2,256]{1,0:T(2,128)S(1)}, u32[]{:S(2)}, u32[]{:S(2)}) %collective-permute-start.45) | collective-permute-done | bytes 2080 | tf_op jit(solution)/shard_map/ppermute | solution.py:23
  275.7 3.6 %collective-permute-done.49 = f32[2,512]{0,1:T(8,128)S(1)} collective-permute-done((f32[2,512]{0,1:T(8,128)S(1)}, f32[2,512]{0,1:T(8,128)S(1)}, u32[]{:S(2)}, u32[]{:S(2)}) %collective-permute-start.49) | collective-permute-done | bytes 4128 | tf_op jit(solution)/shard_map/ppermute | solution.py:23
  (206 shorter events, 108.0 us)
Async XLA Ops:
  0.0 52.8 %collective-permute-start = (f32[2,512]{0,1:T(8,128)S(1)}, f32[2,512]{0,1:T(8,128)S(1)}, u32[]{:S(2)}, u32[]{:S(2)}) collective-permute-start(f32[2,512]{0,1:T(8,128)S(1)} %broadcast.431), channel_id=1, source_target_pairs={{0,4},{4,8},{8,12},{12,16},{16,20},{20,24},{24,28},{1,5},{5,9},{9,... | collective-permute-start | bytes 12296 | tf_op jit(solution)/shard_map/ppermute | solution.py:21
  3.8 52.2 %collective-permute-start.1 = (f32[2,512]{0,1:T(8,128)S(1)}, f32[2,512]{0,1:T(8,128)S(1)}, u32[]{:S(2)}, u32[]{:S(2)}) collective-permute-start(f32[2,512]{0,1:T(8,128)S(1)} %broadcast.431), channel_id=1, source_target_pairs={{4,0},{8,4},{12,8},{16,12},{20,16},{24,20},{28,24},{5,1},{9,5},{13... | collective-permute-start | bytes 12296 | tf_op jit(solution)/shard_map/ppermute | solution.py:23
  8.8 37.4 %collective-permute-start.4 = (f32[2,1,512]{1,2,0:T(8,128)}, f32[2,1,512]{1,2,0:T(8,128)S(1)}, u32[]{:S(2)}, u32[]{:S(2)}) collective-permute-start(f32[2,1,512]{1,2,0:T(8,128)} %get-tuple-element.15), channel_id=1, source_target_pairs={{0,4},{4,8},{8,12},{12,16},{16,20},{20,24},{24,28},{1,5},{5,9},{9,... | collective-permute-start | bytes 12296 | tf_op jit(solution)/shard_map/ppermute | solution.py:21
  13.4 34.8 %collective-permute-start.5 = (f32[2,1,512]{1,2,0:T(8,128)S(1)}, f32[2,1,512]{1,2,0:T(8,128)S(1)}, u32[]{:S(2)}, u32[]{:S(2)}) collective-permute-start(f32[2,1,512]{1,2,0:T(8,128)S(1)} %get-tuple-element.16), channel_id=1, source_target_pairs={{4,0},{8,4},{12,8},{16,12},{20,16},{24,20},{28,24},{5,1},{9,5},{13... | collective-permute-start | bytes 12296 | tf_op jit(solution)/shard_map/ppermute | solution.py:23
  15.3 65.8 %collective-permute-start.8 = (f32[2,256]{1,0:T(2,128)S(1)}, f32[2,256]{1,0:T(2,128)S(1)}, u32[]{:S(2)}, u32[]{:S(2)}) collective-permute-start(f32[2,256]{1,0:T(2,128)S(1)} %broadcast.445), channel_id=1, source_target_pairs={{0,4},{4,8},{8,12},{12,16},{16,20},{20,24},{24,28},{1,5},{5,9},{9,... | collective-permute-start | bytes 6152 | tf_op jit(solution)/shard_map/ppermute | solution.py:21
  46.2 38.9 %collective-permute-start.9 = (f32[2,256]{1,0:T(2,128)S(1)}, f32[2,256]{1,0:T(2,128)S(1)}, u32[]{:S(2)}, u32[]{:S(2)}) collective-permute-start(f32[2,256]{1,0:T(2,128)S(1)} %broadcast.445), channel_id=1, source_target_pairs={{4,0},{8,4},{12,8},{16,12},{20,16},{24,20},{28,24},{5,1},{9,5},{13... | collective-permute-start | bytes 6152 | tf_op jit(solution)/shard_map/ppermute | solution.py:23
  48.1 101.7 %collective-permute-start.20 = (f32[2,128]{1,0:T(2,128)S(1)}, f32[2,128]{1,0:T(2,128)S(1)}, u32[]{:S(2)}, u32[]{:S(2)}) collective-permute-start(f32[2,128]{1,0:T(2,128)S(1)} %broadcast.459), channel_id=1, source_target_pairs={{0,4},{4,8},{8,12},{12,16},{16,20},{20,24},{24,28},{1,5},{5,9},{9,... | collective-permute-start | bytes 3080 | tf_op jit(solution)/shard_map/ppermute | solution.py:21
  56.0 5.4 %collective-permute-start.7 = (f32[2,130,1]{1,2,0:T(1,128)S(1)}, f32[2,130,1]{1,2,0:T(1,128)S(1)}, u32[]{:S(2)}, u32[]{:S(2)}) collective-permute-start(f32[2,130,1]{1,2,0:T(1,128)S(1)} %get-tuple-element.8), channel_id=1, source_target_pairs={{1,0},{2,1},{3,2},{5,4},{6,5},{7,6},{9,8},{10,9},{11,10},{13,12},{... | collective-permute-start | bytes 3128 | tf_op jit(solution)/shard_map/ppermute | solution.py:23
  57.4 5.8 %collective-permute-start.2 = (f32[132,2]{0,1:T(2,128)S(1)}, f32[132,2]{0,1:T(2,128)S(1)}, u32[]{:S(2)}, u32[]{:S(2)}) collective-permute-start(f32[132,2]{0,1:T(2,128)S(1)} %get-tuple-element.14), channel_id=1, source_target_pairs={{0,1},{1,2},{2,3},{4,5},{5,6},{6,7},{8,9},{9,10},{10,11},{12,13},{... | collective-permute-start | bytes 3176 | tf_op jit(solution)/shard_map/ppermute | solution.py:21
  67.5 10.3 %collective-permute-start.12 = (f32[1,512]{0,1:T(8,128)S(1)}, f32[1,512]{0,1:T(8,128)S(1)}, u32[]{:S(2)}, u32[]{:S(2)}) collective-permute-start(f32[1,512]{0,1:T(8,128)S(1)} %get-tuple-element.20), channel_id=1, source_target_pairs={{4,0},{8,4},{12,8},{16,12},{20,16},{24,20},{28,24},{5,1},{9,5},{13... | collective-permute-start | bytes 6152 | tf_op jit(solution)/shard_map/ppermute | solution.py:23
  69.4 10.3 %collective-permute-start.13 = (f32[1,512]{0,1:T(8,128)S(1)}, f32[1,512]{0,1:T(8,128)S(1)}, u32[]{:S(2)}, u32[]{:S(2)}) collective-permute-start(f32[1,512]{0,1:T(8,128)S(1)} %get-tuple-element.19), channel_id=1, source_target_pairs={{0,4},{4,8},{8,12},{12,16},{16,20},{20,24},{24,28},{1,5},{5,9},{9,... | collective-permute-start | bytes 6152 | tf_op jit(solution)/shard_map/ppermute | solution.py:21
  77.8 72.1 %collective-permute-start.21 = (f32[2,128]{1,0:T(2,128)S(1)}, f32[2,128]{1,0:T(2,128)S(1)}, u32[]{:S(2)}, u32[]{:S(2)}) collective-permute-start(f32[2,128]{1,0:T(2,128)S(1)} %broadcast.459), channel_id=1, source_target_pairs={{4,0},{8,4},{12,8},{16,12},{20,16},{24,20},{28,24},{5,1},{9,5},{13... | collective-permute-start | bytes 3080 | tf_op jit(solution)/shard_map/ppermute | solution.py:23
  112.5 11.6 %collective-permute-start.16 = (f32[2,1,256]{2,1,0:T(1,128)S(1)}, f32[2,1,256]{2,1,0:T(1,128)S(1)}, u32[]{:S(2)}, u32[]{:S(2)}) collective-permute-start(f32[2,1,256]{2,1,0:T(1,128)S(1)} %get-tuple-element.23), channel_id=1, source_target_pairs={{0,4},{4,8},{8,12},{12,16},{16,20},{20,24},{24,28},{1,5},{5,9},{9,... | collective-permute-start | bytes 6152 | tf_op jit(solution)/shard_map/ppermute | solution.py:21
  118.1 7.2 %collective-permute-start.17 = (f32[2,1,256]{2,1,0:T(1,128)S(1)}, f32[2,1,256]{2,1,0:T(1,128)S(1)}, u32[]{:S(2)}, u32[]{:S(2)}) collective-permute-start(f32[2,1,256]{2,1,0:T(1,128)S(1)} %get-tuple-element.24), channel_id=1, source_target_pairs={{4,0},{8,4},{12,8},{16,12},{20,16},{24,20},{28,24},{5,1},{9,5},{13... | collective-permute-start | bytes 6152 | tf_op jit(solution)/shard_map/ppermute | solution.py:23
  120.1 9.3 %collective-permute-start.10 = (f32[68,2]{1,0:T(8,128)S(1)}, f32[68,2]{1,0:T(8,128)S(1)}, u32[]{:S(2)}, u32[]{:S(2)}) collective-permute-start(f32[68,2]{1,0:T(8,128)S(1)} %get-tuple-element.30), channel_id=1, source_target_pairs={{0,1},{1,2},{2,3},{4,5},{5,6},{6,7},{8,9},{9,10},{10,11},{12,13},{... | collective-permute-start | bytes 1640 | tf_op jit(solution)/shard_map/ppermute | solution.py:21
  124.1 6.9 %collective-permute-start.11 = (f32[68,2]{1,0:T(8,128)S(1)}, f32[68,2]{1,0:T(8,128)S(1)}, u32[]{:S(2)}, u32[]{:S(2)}) collective-permute-start(f32[68,2]{1,0:T(8,128)S(1)} %get-tuple-element.29), channel_id=1, source_target_pairs={{1,0},{2,1},{3,2},{5,4},{6,5},{7,6},{9,8},{10,9},{11,10},{13,12},{... | collective-permute-start | bytes 1640 | tf_op jit(solution)/shard_map/ppermute | solution.py:23
  125.5 5.6 %collective-permute-start.18 = (f32[2,66,1]{2,1,0:T(8,128)S(1)}, f32[2,66,1]{2,1,0:T(8,128)S(1)}, u32[]{:S(2)}, u32[]{:S(2)}) collective-permute-start(f32[2,66,1]{2,1,0:T(8,128)S(1)} %get-tuple-element.21), channel_id=1, source_target_pairs={{0,1},{1,2},{2,3},{4,5},{5,6},{6,7},{8,9},{9,10},{10,11},{12,13},{... | collective-permute-start | bytes 1592 | tf_op jit(solution)/shard_map/ppermute | solution.py:21
  135.3 8.5 %collective-permute-start.24 = (f32[1,256]{1,0:T(1,128)S(1)}, f32[1,256]{1,0:T(1,128)S(1)}, u32[]{:S(2)}, u32[]{:S(2)}) collective-permute-start(f32[1,256]{1,0:T(1,128)S(1)} %get-tuple-element.36), channel_id=1, source_target_pairs={{4,0},{8,4},{12,8},{16,12},{20,16},{24,20},{28,24},{5,1},{9,5},{13... | collective-permute-start | bytes 3080 | tf_op jit(solution)/shard_map/ppermute | solution.py:23
  137.2 7.2 %collective-permute-start.25 = (f32[1,256]{1,0:T(1,128)S(1)}, f32[1,256]{1,0:T(1,128)S(1)}, u32[]{:S(2)}, u32[]{:S(2)}) collective-permute-start(f32[1,256]{1,0:T(1,128)S(1)} %get-tuple-element.35), channel_id=1, source_target_pairs={{0,4},{4,8},{8,12},{12,16},{16,20},{20,24},{24,28},{1,5},{5,9},{9,... | collective-permute-start | bytes 3080 | tf_op jit(solution)/shard_map/ppermute | solution.py:21
  167.8 13.5 %collective-permute-start.28 = (f32[2,1,128]{2,1,0:T(1,128)S(1)}, f32[2,1,128]{2,1,0:T(1,128)S(1)}, u32[]{:S(2)}, u32[]{:S(2)}) collective-permute-start(f32[2,1,128]{2,1,0:T(1,128)S(1)} %get-tuple-element.43), channel_id=1, source_target_pairs={{0,4},{4,8},{8,12},{12,16},{16,20},{20,24},{24,28},{1,5},{5,9},{9,... | collective-permute-start | bytes 3080 | tf_op jit(solution)/shard_map/ppermute | solution.py:21
  174.0 7.3 %collective-permute-start.29 = (f32[2,1,128]{2,1,0:T(1,128)S(1)}, f32[2,1,128]{2,1,0:T(1,128)S(1)}, u32[]{:S(2)}, u32[]{:S(2)}) collective-permute-start(f32[2,1,128]{2,1,0:T(1,128)S(1)} %get-tuple-element.44), channel_id=1, source_target_pairs={{4,0},{8,4},{12,8},{16,12},{20,16},{24,20},{28,24},{5,1},{9,5},{13... | collective-permute-start | bytes 3080 | tf_op jit(solution)/shard_map/ppermute | solution.py:23
  176.0 10.7 %collective-permute-start.22 = (f32[36,2]{1,0:T(8,128)S(1)}, f32[36,2]{1,0:T(8,128)S(1)}, u32[]{:S(2)}, u32[]{:S(2)}) collective-permute-start(f32[36,2]{1,0:T(8,128)S(1)} %get-tuple-element.50), channel_id=1, source_target_pairs={{0,1},{1,2},{2,3},{4,5},{5,6},{6,7},{8,9},{9,10},{10,11},{12,13},{... | collective-permute-start | bytes 872 | tf_op jit(solution)/shard_map/ppermute | solution.py:21
  180.0 6.7 %collective-permute-start.23 = (f32[36,2]{1,0:T(8,128)S(1)}, f32[36,2]{1,0:T(8,128)S(1)}, u32[]{:S(2)}, u32[]{:S(2)}) collective-permute-start(f32[36,2]{1,0:T(8,128)S(1)} %get-tuple-element.49), channel_id=1, source_target_pairs={{1,0},{2,1},{3,2},{5,4},{6,5},{7,6},{9,8},{10,9},{11,10},{13,12},{... | collective-permute-start | bytes 872 | tf_op jit(solution)/shard_map/ppermute | solution.py:23
  181.4 5.4 %collective-permute-start.30 = (f32[2,34,1]{2,1,0:T(8,128)S(1)}, f32[2,34,1]{2,1,0:T(8,128)S(1)}, u32[]{:S(2)}, u32[]{:S(2)}) collective-permute-start(f32[2,34,1]{2,1,0:T(8,128)S(1)} %get-tuple-element.41), channel_id=1, source_target_pairs={{0,1},{1,2},{2,3},{4,5},{5,6},{6,7},{8,9},{9,10},{10,11},{12,13},{... | collective-permute-start | bytes 824 | tf_op jit(solution)/shard_map/ppermute | solution.py:21
  190.5 8.5 %collective-permute-start.32 = (f32[1,128]{1,0:T(1,128)S(1)}, f32[1,128]{1,0:T(1,128)S(1)}, u32[]{:S(2)}, u32[]{:S(2)}) collective-permute-start(f32[1,128]{1,0:T(1,128)S(1)} %get-tuple-element.56), channel_id=1, source_target_pairs={{4,0},{8,4},{12,8},{16,12},{20,16},{24,20},{28,24},{5,1},{9,5},{13... | collective-permute-start | bytes 1544 | tf_op jit(solution)/shard_map/ppermute | solution.py:23
  192.4 7.2 %collective-permute-start.33 = (f32[1,128]{1,0:T(1,128)S(1)}, f32[1,128]{1,0:T(1,128)S(1)}, u32[]{:S(2)}, u32[]{:S(2)}) collective-permute-start(f32[1,128]{1,0:T(1,128)S(1)} %get-tuple-element.55), channel_id=1, source_target_pairs={{0,4},{4,8},{8,12},{12,16},{16,20},{20,24},{24,28},{1,5},{5,9},{9,... | collective-permute-start | bytes 1544 | tf_op jit(solution)/shard_map/ppermute | solution.py:21
  208.5 8.2 %collective-permute-start.36 = (f32[2,16,64]{2,1,0:T(8,128)S(1)}, f32[2,16,64]{2,1,0:T(8,128)S(1)}, u32[]{:S(2)}, u32[]{:S(2)}) collective-permute-start(f32[2,16,64]{2,1,0:T(8,128)S(1)} %pad_maximum_fusion.80), channel_id=1, source_target_pairs={{0,4},{4,8},{8,12},{12,16},{16,20},{20,24},{24,28},{1,5},{5,9},{9,... | collective-permute-start | bytes 24584 | tf_op jit(solution)/shard_map/ppermute | solution.py:21
  214.7 6.0 %collective-permute-start.37 = (f32[2,16,64]{2,1,0:T(8,128)S(1)}, f32[2,16,64]{2,1,0:T(8,128)S(1)}, u32[]{:S(2)}, u32[]{:S(2)}) collective-permute-start(f32[2,16,64]{2,1,0:T(8,128)S(1)} %pad_maximum_fusion.80), channel_id=1, source_target_pairs={{4,0},{8,4},{12,8},{16,12},{20,16},{24,20},{28,24},{5,1},{9,5},{13... | collective-permute-start | bytes 24584 | tf_op jit(solution)/shard_map/ppermute | solution.py:23
  234.9 5.8 %collective-permute-start.41 = (f32[2,128]{1,0:T(2,128)S(1)}, f32[2,128]{1,0:T(2,128)S(1)}, u32[]{:S(2)}, u32[]{:S(2)}) collective-permute-start(f32[2,128]{1,0:T(2,128)S(1)} %get-tuple-element.52), channel_id=1, source_target_pairs={{4,0},{8,4},{12,8},{16,12},{20,16},{24,20},{28,24},{5,1},{9,5},{13... | collective-permute-start | bytes 3080 | tf_op jit(solution)/shard_map/ppermute | solution.py:23
  252.5 5.8 %collective-permute-start.45 = (f32[2,256]{1,0:T(2,128)S(1)}, f32[2,256]{1,0:T(2,128)S(1)}, u32[]{:S(2)}, u32[]{:S(2)}) collective-permute-start(f32[2,256]{1,0:T(2,128)S(1)} %get-tuple-element.32), channel_id=1, source_target_pairs={{4,0},{8,4},{12,8},{16,12},{20,16},{24,20},{28,24},{5,1},{9,5},{13... | collective-permute-start | bytes 6152 | tf_op jit(solution)/shard_map/ppermute | solution.py:23
  267.3 8.3 %collective-permute-start.48 = (f32[2,512]{0,1:T(8,128)S(1)}, f32[2,512]{0,1:T(8,128)S(1)}, u32[]{:S(2)}, u32[]{:S(2)}) collective-permute-start(f32[2,512]{0,1:T(8,128)S(1)} %get-tuple-element.17), channel_id=1, source_target_pairs={{0,4},{4,8},{8,12},{12,16},{16,20},{20,24},{24,28},{1,5},{5,9},{9,... | collective-permute-start | bytes 12296 | tf_op jit(solution)/shard_map/ppermute | solution.py:21
  270.7 8.6 %collective-permute-start.49 = (f32[2,512]{0,1:T(8,128)S(1)}, f32[2,512]{0,1:T(8,128)S(1)}, u32[]{:S(2)}, u32[]{:S(2)}) collective-permute-start(f32[2,512]{0,1:T(8,128)S(1)} %get-tuple-element.18), channel_id=1, source_target_pairs={{4,0},{8,4},{12,8},{16,12},{20,16},{24,20},{28,24},{5,1},{9,5},{13... | collective-permute-start | bytes 12296 | tf_op jit(solution)/shard_map/ppermute | solution.py:23
  (21 other events, 103.5 us)
where the time goes:
time: 290 us; the launch traced here: 288 us
  starting transfers between devices  152 us (52%)
  local copies, waits for them, and re-layouts  53.5 us (18%)
  waiting for transfers between devices  48.7 us (17%)
  other arithmetic  32.1 us (11%)
    ppermute x26, starting transfers between devices, with_halo(): lax.ppermute(tail, axis, [(i, (i + 1) % count) for i in range(ends)])  110 us
    reshape x4, local copies, waits for them, and re-layouts, restrict(): return field.reshape(height // 2, 2, width // 2, 2).mean(axis=(1, 3))  42.8 us
    ppermute x26, starting transfers between devices, with_halo(): lax.ppermute(head, axis, [((i + 1) % count, i) for i in range(ends)])  41.9 us
    ppermute x26, waiting for transfers between devices, with_halo(): lax.ppermute(head, axis, [((i + 1) % count, i) for i in range(ends)])  41.8 us
    reduce_sum x6, other arithmetic, restrict(): return field.reshape(height // 2, 2, width // 2, 2).mean(axis=(1, 3))  22 us
    ppermute x26, waiting for transfers between devices, with_halo(): lax.ppermute(tail, axis, [(i, (i + 1) % count) for i in range(ends)])  6.94 us
    div x2, local copies, waits for them, and re-layouts, restrict(): return field.reshape(height // 2, 2, width // 2, 2).mean(axis=(1, 3))  6.59 us
  transfers between devices with their start and end apart: 52, of which 18 were waited for; matrix products, arithmetic and copies ran while one was open for 21% of the time, Pallas kernels for 0%

commit v1 on v0

v1 whole, which is shorter than its diff:
```python
import functools

import jax
import jax.numpy as jnp
from jax import lax
from jax.experimental import pallas as pl
from jax.experimental.pallas import tpu as pltpu
from jax.sharding import PartitionSpec as P

BLOCK = 8
NC = 16
LANES = 128
ROWS = 32
NEAR = 128
FAR = 32
damping = 0.8

f32 = jnp.float32
HIGHEST = lax.Precision.HIGHEST


def roll(value, shift, axis):
    return pltpu.roll(value, shift % value.shape[axis], axis)


def around(value, step):
    rows = roll(value, 1, 0) + roll(value, -1, 0)
    return rows + (roll(value, step, 1) + roll(value, -step, 1))


def iota(shape, axis):
    return lax.broadcasted_iota(jnp.int32, shape, axis)


def ones_where(condition):
    return jnp.where(condition, 1.0, 0.0).astype(f32)


def pack_near_far(tiles, near_tile, far_tile, far_lane):
    far = tiles[:, far_tile * LANES : (far_tile + 1) * LANES]
    near = tiles[:, near_tile * LANES : (near_tile + 1) * LANES]
    count = LANES // FAR
    group = tiles.shape[0] // count
    lane = iota((group, LANES), 1) // FAR
    packed = jnp.zeros((group, LANES), f32)
    for g in range(count):
        moved = roll(far[g * group : (g + 1) * group], FAR * g - far_lane, 1)
        packed = jnp.where(lane == g, moved, packed)
    return near, packed


def edges_kernel(right_ref, kappa_ref, ice_ref, reaction_ref, even_ref, odd_ref):
    height, width = right_ref.shape
    blocks = ice_ref.shape
    ice = ice_ref[...].astype(f32)
    spread = ones_where(iota((blocks[1], width), 1) // BLOCK == iota((blocks[1], width), 0))
    repeat = ones_where(iota((height, blocks[0]), 0) // BLOCK == iota((height, blocks[0]), 1))
    ice = jnp.dot(ice, spread, preferred_element_type=f32)
    ice = jnp.dot(repeat, ice, preferred_element_type=f32)
    reaction = kappa_ref[...] * (1.0 + 3.0 * (1.0 - ice))
    reaction_ref[...] = reaction
    tiles = width // LANES
    even = lax.rem(lax.axis_index("gy"), 2) == 0
    size = height + height * FAR // LANES
    for k, field in enumerate((right_ref[...], reaction)):
        to_right = pack_near_far(field, tiles - 1, tiles - 2, LANES - FAR)
        to_left = pack_near_far(field, 0, 1, 0)
        start = k * size
        for a, b in zip(to_right, to_left):
            stop = start + a.shape[0]
            even_ref[start:stop, :] = jnp.where(even, a, b)
            odd_ref[start:stop, :] = jnp.where(even, b, a)
            start = stop


def widen_columns(own, even_msg, odd_msg, even, rows):
    height, width = own.shape
    from_right = jnp.where(even, even_msg, odd_msg)
    from_left = jnp.where(even, odd_msg, even_msg)
    count = LANES // FAR
    group = height // count
    far_right = from_right[height:]
    far_left = from_left[height:]
    pieces = []
    lane = iota((group, LANES), 1)
    for g in range(count):
        if g * group >= rows[1] or (g + 1) * group <= rows[0]:
            continue
        piece = jnp.where(lane < FAR, roll(far_right, -FAR * g, 1), 0.0)
        piece = jnp.where(lane >= LANES - FAR, roll(far_left, LANES - FAR - FAR * g, 1), piece)
        pieces.append(piece)
    far = jnp.concatenate(pieces, axis=0) if len(pieces) > 1 else pieces[0]
    near_left = from_left[rows[0] : rows[1]]
    near_right = from_right[rows[0] : rows[1]]
    return jnp.concatenate([near_left, own[rows[0] : rows[1]], near_right, far], axis=1)


def rows_kernel(right_ref, reaction_ref, even_ref, odd_ref, even_out, odd_out):
    height = right_ref.shape[0]
    even_column = lax.rem(lax.axis_index("gy"), 2) == 0
    even_row = lax.rem(lax.axis_index("gx"), 2) == 0
    size = even_ref.shape[0] // 2
    for k, ref in enumerate((right_ref, reaction_ref)):
        a = even_ref[k * size : (k + 1) * size]
        b = odd_ref[k * size : (k + 1) * size]
        up = widen_columns(ref[...], a, b, even_column, (0, ROWS))
        down = widen_columns(ref[...], a, b, even_column, (height - ROWS, height))
        even_out[k * ROWS : (k + 1) * ROWS] = jnp.where(even_row, down, up)
        odd_out[k * ROWS : (k + 1) * ROWS] = jnp.where(even_row, up, down)


def pair_rows(value, scratch):
    rows, width = value.shape
    pieces = []
    for j in range(width // LANES):
        scratch[j, :rows] = value[:, j * LANES : (j + 1) * LANES]
        first = scratch[j, pl.ds(0, rows // 2, stride=2), :]
        second = scratch[j, pl.ds(1, rows // 2, stride=2), :]
        pieces.append(first + second)
    return jnp.concatenate(pieces, axis=1)


def pair_lanes(value, step):
    lane = iota(value.shape, 1)
    other = jnp.where((lane // step) % 2 == 0, roll(value, -step, 1), roll(value, step, 1))
    return value + other


def double_rows(value, scratch):
    rows, width = value.shape
    pieces = []
    for j in range(width // LANES):
        piece = value[:, j * LANES : (j + 1) * LANES]
        scratch[j, pl.ds(0, rows, stride=2), :] = piece
        scratch[j, pl.ds(1, rows, stride=2), :] = piece
        pieces.append(scratch[j, : 2 * rows])
    return jnp.concatenate(pieces, axis=1)


def keep_post(value, top, rows, ref):
    value = value[top : top + rows]
    width = value.shape[1] - 3 * LANES
    lane = iota((rows, LANES), 1)
    left = value[:, :LANES]
    right = value[:, LANES + width : 2 * LANES + width]
    ref[:, :width] = value[:, LANES : LANES + width]
    ref[:, width:] = jnp.where(lane < LANES // 2, right, left)


def down_kernel(height, width, grid_rows, grid_cols, *refs):
    right_ref, reaction_ref, even_ref, odd_ref, even_rows, odd_rows = refs[:6]
    outs = refs[6:15]
    own_out, even_out, odd_out = refs[15:18]
    scratch = refs[18]
    even_column = lax.rem(lax.axis_index("gy"), 2) == 0
    even_row = lax.rem(lax.axis_index("gx"), 2) == 0
    size = even_ref.shape[0] // 2
    fields = []
    for k, ref in enumerate((right_ref, reaction_ref)):
        a = even_ref[k * size : (k + 1) * size]
        b = odd_ref[k * size : (k + 1) * size]
        own = widen_columns(ref[...], a, b, even_column, (0, height))
        a = even_rows[k * ROWS : (k + 1) * ROWS]
        b = odd_rows[k * ROWS : (k + 1) * ROWS]
        top = jnp.where(even_row, b, a)
        bottom = jnp.where(even_row, a, b)
        fields.append(jnp.concatenate([top, own, bottom], axis=0))
    source, reaction = fields
    total = source.shape[1]
    first_row = lax.axis_index("gx") * height - ROWS
    first_col = lax.axis_index("gy") * width
    col = iota((1, total), 1)
    col = jnp.where(col >= total - FAR, col - total, col) - NEAR + first_col
    col_in = ones_where((col >= 0) & (col < grid_cols))
    margin = ROWS
    for level in range(3):
        rows = source.shape[0]
        row = first_row + iota((rows, 1), 0) * 2**level
        inside = ones_where((row >= 0) & (row < grid_rows)) * col_in
        stiffness = 0.25**level
        step = 2**level
        diagonal = reaction + 4.0 * stiffness
        gain = inside * (damping / diagonal)
        field = gain * source
        field = gain * ((2.0 - damping) * source + stiffness * around(field, step))
        keep = min(margin, 8)
        kept = rows - 2 * (margin - keep)
        for value, ref in zip((field, source, gain), outs[3 * level : 3 * level + 3]):
            keep_post(value, margin - keep, kept, ref)
        residual = source - diagonal * field + stiffness * around(field, step)
        source = pair_rows(residual, scratch)
        reaction = pair_rows(reaction, scratch)
        margin //= 2
        if level < 2:
            source = 0.25 * pair_lanes(source, step)
            reaction = 0.25 * pair_lanes(reaction, step)
    cell = iota((total, LANES), 0)
    step = 4
    target = jnp.where(cell >= total - FAR, cell - total + 8 * LANES, cell) // 8
    valid = (cell % step == 0) & ((cell < total - LANES + FAR) | (cell >= total - FAR))
    gather = ones_where(valid & (target == iota((total, LANES), 1)))
    coarse_rows = source.shape[0]
    for k, value in enumerate((source, reaction)):
        compact = 0.25 * jnp.dot(value, gather, precision=HIGHEST, preferred_element_type=f32)
        own_out[k * coarse_rows : (k + 1) * coarse_rows] = compact
        half = height // 8
        to_next = compact[margin - 1 : margin - 1 + half]
        to_last = compact[margin + 1 : margin + 1 + half]
        even_out[k * half : (k + 1) * half] = jnp.where(even_row, to_next, to_last)
        odd_out[k * half : (k + 1) * half] = jnp.where(even_row, to_last, to_next)


def up_kernel(height, width, grid_rows, grid_cols, *refs):
    posts = refs[:9]
    own_ref, even_ref, odd_ref = refs[9:12]
    out_ref = refs[12]
    scratch, region = refs[13:15]
    even_row = lax.rem(lax.axis_index("gx"), 2) == 0
    half = height // 8
    coarse_rows = own_ref.shape[0] // 2
    margin = (coarse_rows - half) // 2
    lead = 8 + half
    rows = region.shape[1]
    region[...] = jnp.zeros_like(region)
    for k in range(2):
        a = even_ref[k * half : (k + 1) * half]
        b = odd_ref[k * half : (k + 1) * half]
        own = own_ref[k * coarse_rows : (k + 1) * coarse_rows]
        region[k, lead - 1 - half : lead - 1] = jnp.where(even_row, b, a)
        region[k, lead - 1 : lead + half + 1] = own[margin - 1 : margin + half + 1]
        region[k, lead + half + 1 : lead + 2 * half + 1] = jnp.where(even_row, a, b)
    stiffness = 0.25**3
    row = lax.axis_index("gx") * half - lead + iota((rows, LANES), 0)
    col = iota((rows, LANES), 1)
    col = jnp.where(col >= LANES - FAR // 8, col - LANES, col) - NEAR // 8
    col = col + lax.axis_index("gy") * (width // 8)
    inside = (row >= 0) & (row < grid_rows // 8) & (col >= 0) & (col < grid_cols // 8)
    gain = ones_where(inside) * (damping / (region[1] + 4.0 * stiffness))
    field = gain * region[0]
    constant = field
    gain = gain * stiffness
    for sweep in range(NC - 1):
        field = (1.0 - damping) * field + constant + gain * around(field, 1)
    field = field[lead - margin : lead - margin + coarse_rows]
    total = width + LANES
    position = iota((LANES, total), 1)
    position = jnp.where(position >= width + LANES // 2, position - total, position)
    source_lane = (position + NEAR) // 8
    expand = ones_where(source_lane == iota((LANES, total), 0))
    field = jnp.dot(field, expand, precision=HIGHEST, preferred_element_type=f32)
    for level in (2, 1, 0):
        before, source, gain = [ref[...] for ref in posts[3 * level : 3 * level + 3]]
        field = before + double_rows(field, scratch)
        stiffness = 0.25**level
        constant = gain * source
        gain = gain * stiffness
        for sweep in range(2):
            field = (1.0 - damping) * field + constant + gain * around(field, 2**level)
        if level > 0:
            field = field[4 : field.shape[0] - 4]
    out_ref[...] = field[8 : 8 + height, :width]


def swap_pairs(counts, axis):
    nx, ny = counts
    even, odd = [], []
    for i in range(nx):
        for j in range(ny):
            here = i * ny + j
            place = (i, j)[axis]
            last = counts[axis] - 1
            hop = ny if axis == 0 else 1
            even.append((here, here + hop * (1 - 2 * (place % 2))))
            if place in (0, last):
                other = (i * ny + (j ^ 1)) if axis == 0 else ((i ^ 1) * ny + j)
                odd.append((here, other))
            else:
                odd.append((here, here + hop * (2 * (place % 2) - 1)))
    return even, odd


def shape(*dims):
    return jax.ShapeDtypeStruct(dims, f32)


def per_device(counts, right_side, kappa_field, ice_blocks):
    height, width = right_side.shape
    grid_rows, grid_cols = height * counts[0], width * counts[1]
    axes = ("gx", "gy")
    row_even, row_odd = swap_pairs(counts, 0)
    col_even, col_odd = swap_pairs(counts, 1)
    packed = 2 * (height + height * FAR // LANES)
    reaction, even, odd = pl.pallas_call(
        edges_kernel,
        out_shape=(shape(height, width), shape(packed, LANES), shape(packed, LANES)),
        name="edges",
    )(right_side, kappa_field, ice_blocks)
    odd = lax.ppermute(odd, axes, col_odd)
    even = lax.ppermute(even, axes, col_even)
    total = width + 2 * NEAR + LANES
    even_rows, odd_rows = pl.pallas_call(
        rows_kernel,
        out_shape=(shape(2 * ROWS, total), shape(2 * ROWS, total)),
        name="rows",
    )(right_side, reaction, even, odd)
    odd_rows = lax.ppermute(odd_rows, axes, row_odd)
    even_rows = lax.ppermute(even_rows, axes, row_even)
    half = height // 8
    post_shapes = []
    for level in range(3):
        post_shapes += [shape((height >> level) + 16, width + LANES)] * 3
    coarse_rows = half + ROWS // 4
    outs = pl.pallas_call(
        functools.partial(down_kernel, height, width, grid_rows, grid_cols),
        out_shape=(*post_shapes, shape(2 * coarse_rows, LANES), shape(2 * half, LANES), shape(2 * half, LANES)),
        scratch_shapes=[pltpu.VMEM((total // LANES, height + 2 * ROWS, LANES), f32)],
        name="down",
    )(right_side, reaction, even, odd, even_rows, odd_rows)
    posts, own, even, odd = outs[:9], outs[9], outs[10], outs[11]
    odd = lax.ppermute(odd, axes, row_odd)
    even = lax.ppermute(even, axes, row_even)
    return pl.pallas_call(
        functools.partial(up_kernel, height, width, grid_rows, grid_cols),
        out_shape=shape(height, width),
        scratch_shapes=[
            pltpu.VMEM((width // LANES + 1, height + 16, LANES), f32),
            pltpu.VMEM((2, half * 3 + 16, LANES), f32),
        ],
        name="up",
    )(*posts, own, even, odd)


def solution(mesh):
    counts = (mesh.shape["gx"], mesh.shape["gy"])
    return jax.shard_map(
        functools.partial(per_device, counts),
        mesh=mesh,
        in_specs=(P("gx", "gy"),) * 3,
        out_specs=P("gx", "gy"),
        check_vma=False,
    )
```

time: 290 us -> 36.7 us (0.13)
  the two profiles are of different devices: /device:TPU:3 before, /device:TPU:19 now
where the time goes in v1:
time: 36.7 us; the launch traced here: 36.5 us
  waiting for transfers between devices  15.1 us (41%)
  Pallas kernels  13.7 us (37%)
  starting transfers between devices  5.74 us (16%)
  local copies, waits for them, and re-layouts  1.96 us (5%)
    ppermute x1, waiting for transfers between devices, per_device(): odd_rows = lax.ppermute(odd_rows, axes, row_odd)  7.06 us
    pallas_call x1, Pallas kernels, per_device(): pl.pallas_call(functools.partial(down_kernel, height, width, grid_rows, g...  4.92 us
    pallas_call x1, Pallas kernels, per_device(): pl.pallas_call(functools.partial(up_kernel, height, width, grid_rows, gri...  4.64 us
    ppermute x1, waiting for transfers between devices, per_device(): even = lax.ppermute(even, axes, col_even)  3.99 us
    ppermute x1, waiting for transfers between devices, per_device(): odd = lax.ppermute(odd, axes, row_odd)  2.81 us
    pallas_call x1, Pallas kernels, per_device(): pl.pallas_call(edges_kernel, out_shape=(shape(height, width), shape(packe...  2.13 us
    pallas_call x1, Pallas kernels, per_device(): pl.pallas_call(rows_kernel, out_shape=(shape(2 * ROWS, total), shape(2 *...  2 us
    unnamed x12, local copies, waits for them, and re-layouts  1.96 us
  transfers between devices with their start and end apart: 6, of which 5 were waited for; matrix products, arithmetic and copies ran while one was open for 0% of the time, Pallas kernels for 0%

profile of v1, /device:TPU:19, one launch (start us, length us, event | category | flops | bytes accessed | tf_op | source)
XLA Modules:
  0.0 36.5 jit_solution(13968919993974693251)
XLA Ops:
  0.0 2.1 %edges.1 = (f32[128,512]{1,0:T(8,128)}, f32[320,128]{1,0:T(8,128)}, f32[320,128]{1,0:T(8,128)}) custom-call(f32[128,512]{1,0:T(8,128)} %refs_0_.1, f32[128,512]{1,0:T(8,128)} %kappa_ref.1, s32[16,64]{1,0:T(8,128)} %ice_ref.1), custom_call_target="tpu_custom_call" | custom-call | tf_op jit(solution)/shard_map/edges/pallas_call | solution.py:293
  2.1 1.3 %collective-permute-start = (f32[320,128]{1,0:T(8,128)}, f32[320,128]{1,0:T(8,128)S(1)}, u32[]{:S(2)}, u32[]{:S(2)}) collective-permute-start(f32[320,128]{1,0:T(8,128)} %get-tuple-element.23), channel_id=1, source_target_pairs={{0,1},{1,0},{2,3},{3,2},{4,5},{5,4},{6,7},{7,6},{8,9},{9,8},{10,11... | collective-permute-start | bytes 491528 | tf_op jit(solution)/shard_map/ppermute | solution.py:299
  3.4 0.0 collective-permute-start.1
  3.4 4.0 %collective-permute-done.even_ref.refs_2_ = f32[320,128]{1,0:T(8,128)S(1)} collective-permute-done((f32[320,128]{1,0:T(8,128)}, f32[320,128]{1,0:T(8,128)S(1)}, u32[]{:S(2)}, u32[]{:S(2)}) %collective-permute-start) | collective-permute-done | bytes 163872 | tf_op jit(solution)/shard_map/ppermute | solution.py:299
  7.4 0.0 copy-start
  7.4 1.0 %collective-permute-done.1.odd_ref.refs_3_ = f32[320,128]{1,0:T(8,128)S(1)} collective-permute-done((f32[320,128]{1,0:T(8,128)}, f32[320,128]{1,0:T(8,128)S(1)}, u32[]{:S(2)}, u32[]{:S(2)}) %collective-permute-start.1) | collective-permute-done | bytes 163872 | tf_op jit(solution)/shard_map/ppermute | solution.py:298
  8.4 0.0 copy-start.1
  8.4 0.0 copy-done
  8.4 0.7 %copy-done.1 = f32[320,128]{1,0:T(8,128)} copy-done((f32[320,128]{1,0:T(8,128)}, f32[320,128]{1,0:T(8,128)S(1)}, u32[]{:S(2)}) %copy-start.1) | copy-done | bytes 163864
  9.1 2.0 %rows.1 = (f32[64,896]{1,0:T(8,128)}, f32[64,896]{1,0:T(8,128)}) custom-call(f32[128,512]{1,0:T(8,128)} %refs_0_.1, f32[128,512]{1,0:T(8,128)} %get-tuple-element.22.reaction_ref.refs_1_, f32[320,128]{1,0:T(8,128)} %copy-done, f32[320,128]{1,0:T(8,128)} %copy-done.1), custom_call_target="tpu_custom_call" | custom-call | tf_op jit(solution)/shard_map/rows/pallas_call | solution.py:301
  11.1 1.8 %collective-permute-start.2 = (f32[64,896]{1,0:T(8,128)}, f32[64,896]{1,0:T(8,128)S(1)}, u32[]{:S(2)}, u32[]{:S(2)}) collective-permute-start(f32[64,896]{1,0:T(8,128)} %get-tuple-element.25), channel_id=1, source_target_pairs={{0,4},{1,5},{2,6},{3,7},{4,0},{5,1},{6,2},{7,3},{8,12},{9,13},{10,... | collective-permute-start | bytes 688136 | tf_op jit(solution)/shard_map/ppermute | solution.py:307
  12.9 1.1 %collective-permute-start.3 = (f32[64,896]{1,0:T(8,128)}, f32[64,896]{1,0:T(8,128)S(1)}, u32[]{:S(2)}, u32[]{:S(2)}) collective-permute-start(f32[64,896]{1,0:T(8,128)} %get-tuple-element.26), channel_id=1, source_target_pairs={{0,1},{1,0},{2,3},{3,2},{4,8},{5,9},{6,10},{7,11},{8,4},{9,5},{10,... | collective-permute-start | bytes 688136 | tf_op jit(solution)/shard_map/ppermute | solution.py:306
  14.0 0.2 collective-permute-done.2.refs_4_
  14.2 0.0 copy-start.2
  14.2 7.1 %collective-permute-done.3.refs_5_ = f32[64,896]{1,0:T(8,128)S(1)} collective-permute-done((f32[64,896]{1,0:T(8,128)}, f32[64,896]{1,0:T(8,128)S(1)}, u32[]{:S(2)}, u32[]{:S(2)}) %collective-permute-start.3) | collective-permute-done | bytes 229408 | tf_op jit(solution)/shard_map/ppermute | solution.py:306
  21.3 0.0 copy-done.2
  21.3 0.0 copy-start.3
  21.3 0.7 %copy-done.3 = f32[64,896]{1,0:T(8,128)} copy-done((f32[64,896]{1,0:T(8,128)}, f32[64,896]{1,0:T(8,128)S(1)}, u32[]{:S(2)}) %copy-start.3) | copy-done | bytes 229400
  22.0 4.9 %down.1 = (f32[144,640]{1,0:T(8,128)}, f32[144,640]{1,0:T(8,128)}, f32[144,640]{1,0:T(8,128)}, f32[80,640]{1,0:T(8,128)}, f32[80,640]{1,0:T(8,128)}, /*index=5*/...) custom-call(f32[128,512]{1,0:T(8,128)} %refs_0_.1, ...), custom_call_target="tpu_custom_call" | custom-call | tf_op jit(solution)/shard_map/down/pallas_call | solution.py:313
  26.9 0.0 collective-permute-start.4
  26.9 1.5 %collective-permute-start.5 = (f32[32,128]{1,0:T(8,128)}, f32[32,128]{1,0:T(8,128)S(1)}, u32[]{:S(2)}, u32[]{:S(2)}) collective-permute-start(f32[32,128]{1,0:T(8,128)} %get-tuple-element.38), channel_id=1, source_target_pairs={{0,1},{1,0},{2,3},{3,2},{4,8},{5,9},{6,10},{7,11},{8,4},{9,5},{10,... | collective-permute-start | bytes 49160 | tf_op jit(solution)/shard_map/ppermute | solution.py:320
  28.4 0.0 collective-permute-done.4.refs_10_
  28.5 0.0 copy-start.4
  28.5 2.8 %collective-permute-done.5.refs_11_ = f32[32,128]{1,0:T(8,128)S(1)} collective-permute-done((f32[32,128]{1,0:T(8,128)}, f32[32,128]{1,0:T(8,128)S(1)}, u32[]{:S(2)}, u32[]{:S(2)}) %collective-permute-start.5) | collective-permute-done | bytes 16416 | tf_op jit(solution)/shard_map/ppermute | solution.py:320
  31.3 0.0 copy-start.5
  31.3 0.0 copy-done.4
  31.3 0.6 %copy-done.5 = f32[32,128]{1,0:T(8,128)} copy-done((f32[32,128]{1,0:T(8,128)}, f32[32,128]{1,0:T(8,128)S(1)}, u32[]{:S(2)}) %copy-start.5) | copy-done | bytes 16408
  31.9 4.6 %up.1 = f32[128,512]{1,0:T(8,128)} custom-call(f32[144,640]{1,0:T(8,128)} %get-tuple-element.27.refs_0_, f32[144,640]{1,0:T(8,128)} %get-tuple-element.28.refs_1_, f32[144,640]{1,0:T(8,128)} %get-tuple-element.29.refs_2_, f32[80,640]{1,0:T(8,128)} %get-tuple-element.30.refs_3_, f32[80,640]{1,0:T(8,128)} %get-tuple-element.31.refs_4_, ...), custom_call_target="tpu_custom_call" | custom-call | tf_op jit(solution)/shard_map/up/pallas_call | solution.py:322
Async XLA Ops:
  2.1 5.3 %collective-permute-start = (f32[320,128]{1,0:T(8,128)}, f32[320,128]{1,0:T(8,128)S(1)}, u32[]{:S(2)}, u32[]{:S(2)}) collective-permute-start(f32[320,128]{1,0:T(8,128)} %get-tuple-element.23), channel_id=1, source_target_pairs={{0,1},{1,0},{2,3},{3,2},{4,5},{5,4},{6,7},{7,6},{8,9},{9,8},{10,11... | collective-permute-start | bytes 491528 | tf_op jit(solution)/shard_map/ppermute | solution.py:299
  3.4 5.0 %collective-permute-start.1 = (f32[320,128]{1,0:T(8,128)}, f32[320,128]{1,0:T(8,128)S(1)}, u32[]{:S(2)}, u32[]{:S(2)}) collective-permute-start(f32[320,128]{1,0:T(8,128)} %get-tuple-element.24), channel_id=1, source_target_pairs={{0,4},{1,2},{2,1},{3,7},{4,0},{5,6},{6,5},{7,3},{8,12},{9,10},{10,... | collective-permute-start | bytes 491528 | tf_op jit(solution)/shard_map/ppermute | solution.py:298
  7.4 1.0 %copy-start = (f32[320,128]{1,0:T(8,128)}, f32[320,128]{1,0:T(8,128)S(1)}, u32[]{:S(2)}) copy-start(f32[320,128]{1,0:T(8,128)S(1)} %collective-permute-done.even_ref.refs_2_) | copy-start | bytes 491524
  8.4 0.7 %copy-start.1 = (f32[320,128]{1,0:T(8,128)}, f32[320,128]{1,0:T(8,128)S(1)}, u32[]{:S(2)}) copy-start(f32[320,128]{1,0:T(8,128)S(1)} %collective-permute-done.1.odd_ref.refs_3_) | copy-start | bytes 491524
  11.1 3.1 %collective-permute-start.2 = (f32[64,896]{1,0:T(8,128)}, f32[64,896]{1,0:T(8,128)S(1)}, u32[]{:S(2)}, u32[]{:S(2)}) collective-permute-start(f32[64,896]{1,0:T(8,128)} %get-tuple-element.25), channel_id=1, source_target_pairs={{0,4},{1,5},{2,6},{3,7},{4,0},{5,1},{6,2},{7,3},{8,12},{9,13},{10,... | collective-permute-start | bytes 688136 | tf_op jit(solution)/shard_map/ppermute | solution.py:307
  12.9 8.4 %collective-permute-start.3 = (f32[64,896]{1,0:T(8,128)}, f32[64,896]{1,0:T(8,128)S(1)}, u32[]{:S(2)}, u32[]{:S(2)}) collective-permute-start(f32[64,896]{1,0:T(8,128)} %get-tuple-element.26), channel_id=1, source_target_pairs={{0,1},{1,0},{2,3},{3,2},{4,8},{5,9},{6,10},{7,11},{8,4},{9,5},{10,... | collective-permute-start | bytes 688136 | tf_op jit(solution)/shard_map/ppermute | solution.py:306
  14.2 7.1 %copy-start.2 = (f32[64,896]{1,0:T(8,128)}, f32[64,896]{1,0:T(8,128)S(1)}, u32[]{:S(2)}) copy-start(f32[64,896]{1,0:T(8,128)S(1)} %collective-permute-done.2.refs_4_) | copy-start | bytes 688132
  21.3 0.7 %copy-start.3 = (f32[64,896]{1,0:T(8,128)}, f32[64,896]{1,0:T(8,128)S(1)}, u32[]{:S(2)}) copy-start(f32[64,896]{1,0:T(8,128)S(1)} %collective-permute-done.3.refs_5_) | copy-start | bytes 688132
  26.9 1.5 %collective-permute-start.4 = (f32[32,128]{1,0:T(8,128)}, f32[32,128]{1,0:T(8,128)S(1)}, u32[]{:S(2)}, u32[]{:S(2)}) collective-permute-start(f32[32,128]{1,0:T(8,128)} %get-tuple-element.37), channel_id=1, source_target_pairs={{0,4},{1,5},{2,6},{3,7},{4,0},{5,1},{6,2},{7,3},{8,12},{9,13},{10,... | collective-permute-start | bytes 49160 | tf_op jit(solution)/shard_map/ppermute | solution.py:321
  26.9 4.3 %collective-permute-start.5 = (f32[32,128]{1,0:T(8,128)}, f32[32,128]{1,0:T(8,128)S(1)}, u32[]{:S(2)}, u32[]{:S(2)}) collective-permute-start(f32[32,128]{1,0:T(8,128)} %get-tuple-element.38), channel_id=1, source_target_pairs={{0,1},{1,0},{2,3},{3,2},{4,8},{5,9},{6,10},{7,11},{8,4},{9,5},{10,... | collective-permute-start | bytes 49160 | tf_op jit(solution)/shard_map/ppermute | solution.py:320
  28.5 2.8 %copy-start.4 = (f32[32,128]{1,0:T(8,128)}, f32[32,128]{1,0:T(8,128)S(1)}, u32[]{:S(2)}) copy-start(f32[32,128]{1,0:T(8,128)S(1)} %collective-permute-done.4.refs_10_) | copy-start | bytes 49156
  31.3 0.6 %copy-start.5 = (f32[32,128]{1,0:T(8,128)}, f32[32,128]{1,0:T(8,128)S(1)}, u32[]{:S(2)}) copy-start(f32[32,128]{1,0:T(8,128)S(1)} %collective-permute-done.5.refs_11_) | copy-start | bytes 49156

commit v2 on v1

--- a/solution.py
+++ b/solution.py
@@ -13,6 +13,7 @@
 ROWS = 32
 NEAR = 128
 FAR = 32
+VMEM_BYTES = 12 * 2**20
 damping = 0.8
 
 f32 = jnp.float32
@@ -49,18 +50,28 @@
     return near, packed
 
 
-def edges_kernel(right_ref, kappa_ref, ice_ref, reaction_ref, even_ref, odd_ref):
+def edges_kernel(*refs):
+    ins, right_ref, reaction_ref, even_ref, odd_ref, rows_ref = refs[:3], *refs[3:8]
+    kappa_ref, ice_ref, sems = refs[8:11]
+    copies = []
+    for k, (src, dst) in enumerate(zip(ins, (right_ref, kappa_ref, ice_ref))):
+        copies.append(pltpu.make_async_copy(src, dst, sems.at[k]))
+    for copy in copies:
+        copy.start()
     height, width = right_ref.shape
     blocks = ice_ref.shape
-    ice = ice_ref[...].astype(f32)
     spread = ones_where(iota((blocks[1], width), 1) // BLOCK == iota((blocks[1], width), 0))
     repeat = ones_where(iota((height, blocks[0]), 0) // BLOCK == iota((height, blocks[0]), 1))
+    for copy in copies:
+        copy.wait()
+    ice = ice_ref[...].astype(f32)
     ice = jnp.dot(ice, spread, preferred_element_type=f32)
     ice = jnp.dot(repeat, ice, preferred_element_type=f32)
     reaction = kappa_ref[...] * (1.0 + 3.0 * (1.0 - ice))
     reaction_ref[...] = reaction
     tiles = width // LANES
     even = lax.rem(lax.axis_index("gy"), 2) == 0
+    even_row = lax.rem(lax.axis_index("gx"), 2) == 0
     size = height + height * FAR // LANES
     for k, field in enumerate((right_ref[...], reaction)):
         to_right = pack_near_far(field, tiles - 1, tiles - 2, LANES - FAR)
@@ -71,6 +82,7 @@
             even_ref[start:stop, :] = jnp.where(even, a, b)
             odd_ref[start:stop, :] = jnp.where(even, b, a)
             start = stop
+        rows_ref[k * ROWS : (k + 1) * ROWS] = jnp.where(even_row, field[:ROWS], field[height - ROWS :])
 
 
 def widen_columns(own, even_msg, odd_msg, even, rows):
@@ -95,18 +107,24 @@
     return jnp.concatenate([near_left, own[rows[0] : rows[1]], near_right, far], axis=1)
 
 
-def rows_kernel(right_ref, reaction_ref, even_ref, odd_ref, even_out, odd_out):
-    height = right_ref.shape[0]
+def rows_kernel(right_ref, reaction_ref, even_ref, odd_ref, unread_ref, even_out, odd_out):
+    height, width = right_ref.shape
     even_column = lax.rem(lax.axis_index("gy"), 2) == 0
     even_row = lax.rem(lax.axis_index("gx"), 2) == 0
     size = even_ref.shape[0] // 2
+    far = []
     for k, ref in enumerate((right_ref, reaction_ref)):
         a = even_ref[k * size : (k + 1) * size]
         b = odd_ref[k * size : (k + 1) * size]
         up = widen_columns(ref[...], a, b, even_column, (0, ROWS))
         down = widen_columns(ref[...], a, b, even_column, (height - ROWS, height))
         even_out[k * ROWS : (k + 1) * ROWS] = jnp.where(even_row, down, up)
-        odd_out[k * ROWS : (k + 1) * ROWS] = jnp.where(even_row, up, down)
+        odd = jnp.where(even_row, up, down)
+        odd_out[:, 2 * k * LANES : (2 * k + 1) * LANES] = odd[:, :LANES]
+        odd_out[:, (2 * k + 1) * LANES : (2 * k + 2) * LANES] = odd[:, width + LANES : width + 2 * LANES]
+        far.append(odd[:, width + 2 * LANES :])
+    lane = iota((ROWS, LANES), 1)
+    odd_out[:, 4 * LANES :] = jnp.where((lane >= FAR) & (lane < LANES - FAR), roll(far[1], LANES // 2, 1), far[0])
 
 
 def pair_rows(value, scratch):
@@ -148,10 +166,10 @@
 
 
 def down_kernel(height, width, grid_rows, grid_cols, *refs):
-    right_ref, reaction_ref, even_ref, odd_ref, even_rows, odd_rows = refs[:6]
-    outs = refs[6:15]
-    own_out, even_out, odd_out = refs[15:18]
-    scratch = refs[18]
+    right_ref, reaction_ref, even_ref, odd_ref, even_rows, odd_rows, odd_corners = refs[:7]
+    outs = refs[7:16]
+    own_out, even_out, odd_out = refs[16:19]
+    scratch = refs[19]
     even_column = lax.rem(lax.axis_index("gy"), 2) == 0
     even_row = lax.rem(lax.axis_index("gx"), 2) == 0
     size = even_ref.shape[0] // 2
@@ -161,7 +179,18 @@
         b = odd_ref[k * size : (k + 1) * size]
         own = widen_columns(ref[...], a, b, even_column, (0, height))
         a = even_rows[k * ROWS : (k + 1) * ROWS]
-        b = odd_rows[k * ROWS : (k + 1) * ROWS]
+        far = odd_corners[:, 4 * LANES :]
+        if k == 1:
+            far = roll(far, LANES // 2, 1)
+        b = jnp.concatenate(
+            [
+                odd_corners[:, 2 * k * LANES : (2 * k + 1) * LANES],
+                odd_rows[k * ROWS : (k + 1) * ROWS],
+                odd_corners[:, (2 * k + 1) * LANES : (2 * k + 2) * LANES],
+                far,
+            ],
+            axis=1,
+        )
         top = jnp.where(even_row, b, a)
         bottom = jnp.where(even_row, a, b)
         fields.append(jnp.concatenate([top, own, bottom], axis=0))
@@ -272,13 +301,17 @@
             hop = ny if axis == 0 else 1
             even.append((here, here + hop * (1 - 2 * (place % 2))))
             if place in (0, last):
-                other = (i * ny + (j ^ 1)) if axis == 0 else ((i ^ 1) * ny + j)
+                other = ((last - i) * ny + j) if axis == 0 else ((i ^ 1) * ny + j)
                 odd.append((here, other))
             else:
                 odd.append((here, here + hop * (2 * (place % 2) - 1)))
     return even, odd
 
 
+def params():
+    return pltpu.CompilerParams(vmem_limit_bytes=VMEM_BYTES)
+
+
 def shape(*dims):
     return jax.ShapeDtypeStruct(dims, f32)
 
@@ -287,23 +320,41 @@
     height, width = right_side.shape
     grid_rows, grid_cols = height * counts[0], width * counts[1]
     axes = ("gx", "gy")
+    right_side, kappa_field, ice_blocks = [
+        pltpu.with_memory_space_constraint(x, pltpu.HBM) for x in (right_side, kappa_field, ice_blocks)
+    ]
     row_even, row_odd = swap_pairs(counts, 0)
     col_even, col_odd = swap_pairs(counts, 1)
     packed = 2 * (height + height * FAR // LANES)
-    reaction, even, odd = pl.pallas_call(
+    right_side, reaction, even, odd, odd_rows = pl.pallas_call(
         edges_kernel,
-        out_shape=(shape(height, width), shape(packed, LANES), shape(packed, LANES)),
+        out_shape=(
+            shape(height, width),
+            shape(height, width),
+            shape(packed, LANES),
+            shape(packed, LANES),
+            shape(2 * ROWS, width),
+        ),
+        in_specs=[pl.BlockSpec(memory_space=pltpu.HBM)] * 3,
+        scratch_shapes=[
+            pltpu.VMEM((height, width), f32),
+            pltpu.VMEM(ice_blocks.shape, jnp.int32),
+            pltpu.SemaphoreType.DMA((3,)),
+        ],
+        compiler_params=params(),
         name="edges",
     )(right_side, kappa_field, ice_blocks)
+    odd_rows = lax.ppermute(odd_rows, axes, row_odd)
     odd = lax.ppermute(odd, axes, col_odd)
     even = lax.ppermute(even, axes, col_even)
     total = width + 2 * NEAR + LANES
-    even_rows, odd_rows = pl.pallas_call(
+    even_rows, odd_corners = pl.pallas_call(
         rows_kernel,
-        out_shape=(shape(2 * ROWS, total), shape(2 * ROWS, total)),
+        out_shape=(shape(2 * ROWS, total), shape(ROWS, 5 * LANES)),
+        compiler_params=params(),
         name="rows",
-    )(right_side, reaction, even, odd)
-    odd_rows = lax.ppermute(odd_rows, axes, row_odd)
+    )(right_side, reaction, even, odd, odd_rows)
+    odd_corners = lax.ppermute(odd_corners, axes, row_odd)
     even_rows = lax.ppermute(even_rows, axes, row_even)
     half = height // 8
     post_shapes = []
@@ -314,8 +365,9 @@
         functools.partial(down_kernel, height, width, grid_rows, grid_cols),
         out_shape=(*post_shapes, shape(2 * coarse_rows, LANES), shape(2 * half, LANES), shape(2 * half, LANES)),
         scratch_shapes=[pltpu.VMEM((total // LANES, height + 2 * ROWS, LANES), f32)],
+        compiler_params=params(),
         name="down",
-    )(right_side, reaction, even, odd, even_rows, odd_rows)
+    )(right_side, reaction, even, odd, even_rows, odd_rows, odd_corners)
     posts, own, even, odd = outs[:9], outs[9], outs[10], outs[11]
     odd = lax.ppermute(odd, axes, row_odd)
     even = lax.ppermute(even, axes, row_even)
@@ -326,6 +378,7 @@
             pltpu.VMEM((width // LANES + 1, height + 16, LANES), f32),
             pltpu.VMEM((2, half * 3 + 16, LANES), f32),
         ],
+        compiler_params=params(),
         name="up",
     )(*posts, own, even, odd)
 

time: 36.7 us -> 27.5 us (0.75)
  the two profiles are of different devices: /device:TPU:19 before, /device:TPU:8 now
where the time goes in v2:
time: 27.5 us; the launch traced here: 27.4 us
  waiting for transfers between devices  13.4 us (49%)
  Pallas kernels  7.73 us (28%)
  starting transfers between devices  6.19 us (23%)
    ppermute x1, waiting for transfers between devices, per_device(): odd_rows = lax.ppermute(odd_rows, axes, row_odd)  5.27 us
    ppermute x1, waiting for transfers between devices, per_device(): odd_corners = lax.ppermute(odd_corners, axes, row_odd)  4.42 us
    ppermute x1, starting transfers between devices, per_device(): odd = lax.ppermute(odd, axes, col_odd)  3.14 us
    pallas_call x1, Pallas kernels, per_device(): pl.pallas_call(functools.partial(up_kernel, height, width, grid_rows, gri...  3.11 us
    pallas_call x1, Pallas kernels, per_device(): pl.pallas_call(functools.partial(down_kernel, height, width, grid_rows, g...  3.05 us
    ppermute x1, waiting for transfers between devices, per_device(): odd = lax.ppermute(odd, axes, row_odd)  2.96 us
    pallas_call x1, Pallas kernels, per_device(): pl.pallas_call(edges_kernel, out_shape=(shape(height, width), shape(heigh...  1.41 us
    ppermute x1, starting transfers between devices, per_device(): odd_rows = lax.ppermute(odd_rows, axes, row_odd)  1.33 us
  transfers between devices with their start and end apart: 7, of which 4 were waited for; matrix products, arithmetic and copies ran while one was open for 0% of the time, Pallas kernels for 0%

profile of v2, /device:TPU:8, one launch (start us, length us, event | category | flops | bytes accessed | tf_op | source)
XLA Modules:
  0.0 27.4 jit_solution(2955385240549966081)
XLA Ops:
  0.0 1.4 %edges.1 = (f32[128,512]{1,0:T(8,128)S(1)}, f32[128,512]{1,0:T(8,128)S(1)}, f32[320,128]{1,0:T(8,128)S(1)}, f32[320,128]{1,0:T(8,128)S(1)}, f32[64,512]{1,0:T(8,128)S(1)}) custom-call(f32[128,512]{1,0:T(8,128)} %refs_0_.1, f32[128,512]{1,0:T(8,128)} %refs_1_.1, s32[16,64]{1,0:T(8,128)} %refs_2_.1), custom_call_target="tpu_custom_call" | custom-call | tf_op jit(solution)/shard_map/edges/pallas_call | solution.py:329
  1.4 0.1 collective-permute-start
  1.5 3.1 %collective-permute-start.1 = (f32[320,128]{1,0:T(8,128)S(1)}, f32[320,128]{1,0:T(8,128)S(1)}, u32[]{:S(2)}, u32[]{:S(2)}) collective-permute-start(f32[320,128]{1,0:T(8,128)S(1)} %get-tuple-element.27), channel_id=1, source_target_pairs={{0,4},{1,2},{2,1},{3,7},{4,0},{5,6},{6,5},{7,3},{8,12},{9,10},{10,... | collective-permute-start | bytes 491528 | tf_op jit(solution)/shard_map/ppermute | solution.py:348
  4.6 1.3 %collective-permute-start.2 = (f32[64,512]{1,0:T(8,128)S(1)}, f32[64,512]{1,0:T(8,128)S(1)}, u32[]{:S(2)}, u32[]{:S(2)}) collective-permute-start(f32[64,512]{1,0:T(8,128)S(1)} %get-tuple-element.28), channel_id=1, source_target_pairs={{0,28},{1,29},{2,30},{3,31},{4,8},{5,9},{6,10},{7,11},{8,4},{9,5},... | collective-permute-start | bytes 393224 | tf_op jit(solution)/shard_map/ppermute | solution.py:347
  6.0 5.3 %collective-permute-done.2.unread_ref.refs_5_ = f32[64,512]{1,0:T(8,128)S(1)} collective-permute-done((f32[64,512]{1,0:T(8,128)S(1)}, f32[64,512]{1,0:T(8,128)S(1)}, u32[]{:S(2)}, u32[]{:S(2)}) %collective-permute-start.2) | collective-permute-done | bytes 131104 | tf_op jit(solution)/shard_map/ppermute | solution.py:347
  11.2 0.0 collective-permute-done.even_ref.refs_2_
  11.2 0.0 collective-permute-done.1.odd_ref.refs_3_
  11.2 0.2 rows.1
  11.4 0.0 collective-permute-start.3
  11.4 1.2 %collective-permute-start.4 = (f32[32,640]{1,0:T(8,128)S(1)}, f32[32,640]{1,0:T(8,128)S(1)}, u32[]{:S(2)}, u32[]{:S(2)}) collective-permute-start(f32[32,640]{1,0:T(8,128)S(1)} %get-tuple-element.30), channel_id=1, source_target_pairs={{0,28},{1,29},{2,30},{3,31},{4,8},{5,9},{6,10},{7,11},{8,4},{9,5},... | collective-permute-start | bytes 245768 | tf_op jit(solution)/shard_map/ppermute | solution.py:357
  12.6 4.4 %collective-permute-done.4.refs_6_ = f32[32,640]{1,0:T(8,128)S(1)} collective-permute-done((f32[32,640]{1,0:T(8,128)S(1)}, f32[32,640]{1,0:T(8,128)S(1)}, u32[]{:S(2)}, u32[]{:S(2)}) %collective-permute-start.4) | collective-permute-done | bytes 81952 | tf_op jit(solution)/shard_map/ppermute | solution.py:357
  17.0 0.0 collective-permute-done.3.refs_4_
  17.0 3.0 %down.1 = (f32[144,640]{1,0:T(8,128)S(1)}, f32[144,640]{1,0:T(8,128)S(1)}, f32[144,640]{1,0:T(8,128)S(1)}, f32[80,640]{1,0:T(8,128)S(1)}, f32[80,640]{1,0:T(8,12...) custom-call(f32[128,512]{1,0:T(8,128)S(1)} %get-tuple-element.24.rig, ...), custom_call_target="tpu_custom_call" | custom-call | tf_op jit(solution)/shard_map/down/pallas_call | solution.py:364
  20.0 0.1 collective-permute-start.5
  20.1 0.4 %collective-permute-start.6 = (f32[32,128]{1,0:T(8,128)S(1)}, f32[32,128]{1,0:T(8,128)S(1)}, u32[]{:S(2)}, u32[]{:S(2)}) collective-permute-start(f32[32,128]{1,0:T(8,128)S(1)} %get-tuple-element.42), channel_id=1, source_target_pairs={{0,28},{1,29},{2,30},{3,31},{4,8},{5,9},{6,10},{7,11},{8,4},{9,5},... | collective-permute-start | bytes 49160 | tf_op jit(solution)/shard_map/ppermute | solution.py:372
  20.5 0.8 %collective-permute-done.5.refs_10_ = f32[32,128]{1,0:T(8,128)S(1)} collective-permute-done((f32[32,128]{1,0:T(8,128)S(1)}, f32[32,128]{1,0:T(8,128)S(1)}, u32[]{:S(2)}, u32[]{:S(2)}) %collective-permute-start.5) | collective-permute-done | bytes 16416 | tf_op jit(solution)/shard_map/ppermute | solution.py:373
  21.3 3.0 %collective-permute-done.6.refs_11_ = f32[32,128]{1,0:T(8,128)S(1)} collective-permute-done((f32[32,128]{1,0:T(8,128)S(1)}, f32[32,128]{1,0:T(8,128)S(1)}, u32[]{:S(2)}, u32[]{:S(2)}) %collective-permute-start.6) | collective-permute-done | bytes 16416 | tf_op jit(solution)/shard_map/ppermute | solution.py:372
  24.3 3.1 %up.1 = f32[128,512]{1,0:T(8,128)} custom-call(f32[144,640]{1,0:T(8,128)S(1)} %get-tuple-element.31.refs_0_, f32[144,640]{1,0:T(8,128)S(1)} %get-tuple-element.32.refs_1_, f32[144,640]{1,0:T(8,128)S(1)} %get-tuple-element.33.refs_2_, f32[80,640]{1,0:T(8,128)S(1)} %get-tuple-element.34.refs_3_, f32[80,640]{1,0:T(8,128)S(1)} %get-tuple-element.35.refs_4_, ...), custom_call_target="tpu_custom_call" | custom-call | tf_op jit(solution)/shard_map/up/pallas_call | solution.py:374
Async XLA Ops:
  1.4 9.8 %collective-permute-start = (f32[320,128]{1,0:T(8,128)S(1)}, f32[320,128]{1,0:T(8,128)S(1)}, u32[]{:S(2)}, u32[]{:S(2)}) collective-permute-start(f32[320,128]{1,0:T(8,128)S(1)} %get-tuple-element.26), channel_id=1, source_target_pairs={{0,1},{1,0},{2,3},{3,2},{4,5},{5,4},{6,7},{7,6},{8,9},{9,8},{10,11... | collective-permute-start | bytes 491528 | tf_op jit(solution)/shard_map/ppermute | solution.py:349
  1.5 9.7 %collective-permute-start.1 = (f32[320,128]{1,0:T(8,128)S(1)}, f32[320,128]{1,0:T(8,128)S(1)}, u32[]{:S(2)}, u32[]{:S(2)}) collective-permute-start(f32[320,128]{1,0:T(8,128)S(1)} %get-tuple-element.27), channel_id=1, source_target_pairs={{0,4},{1,2},{2,1},{3,7},{4,0},{5,6},{6,5},{7,3},{8,12},{9,10},{10,... | collective-permute-start | bytes 491528 | tf_op jit(solution)/shard_map/ppermute | solution.py:348
  4.6 6.6 %collective-permute-start.2 = (f32[64,512]{1,0:T(8,128)S(1)}, f32[64,512]{1,0:T(8,128)S(1)}, u32[]{:S(2)}, u32[]{:S(2)}) collective-permute-start(f32[64,512]{1,0:T(8,128)S(1)} %get-tuple-element.28), channel_id=1, source_target_pairs={{0,28},{1,29},{2,30},{3,31},{4,8},{5,9},{6,10},{7,11},{8,4},{9,5},... | collective-permute-start | bytes 393224 | tf_op jit(solution)/shard_map/ppermute | solution.py:347
  11.4 5.6 %collective-permute-start.3 = (f32[64,896]{1,0:T(8,128)S(1)}, f32[64,896]{1,0:T(8,128)S(1)}, u32[]{:S(2)}, u32[]{:S(2)}) collective-permute-start(f32[64,896]{1,0:T(8,128)S(1)} %get-tuple-element.29), channel_id=1, source_target_pairs={{0,4},{1,5},{2,6},{3,7},{4,0},{5,1},{6,2},{7,3},{8,12},{9,13},{10,... | collective-permute-start | bytes 688136 | tf_op jit(solution)/shard_map/ppermute | solution.py:358
  11.4 5.6 %collective-permute-start.4 = (f32[32,640]{1,0:T(8,128)S(1)}, f32[32,640]{1,0:T(8,128)S(1)}, u32[]{:S(2)}, u32[]{:S(2)}) collective-permute-start(f32[32,640]{1,0:T(8,128)S(1)} %get-tuple-element.30), channel_id=1, source_target_pairs={{0,28},{1,29},{2,30},{3,31},{4,8},{5,9},{6,10},{7,11},{8,4},{9,5},... | collective-permute-start | bytes 245768 | tf_op jit(solution)/shard_map/ppermute | solution.py:357
  20.0 1.2 %collective-permute-start.5 = (f32[32,128]{1,0:T(8,128)S(1)}, f32[32,128]{1,0:T(8,128)S(1)}, u32[]{:S(2)}, u32[]{:S(2)}) collective-permute-start(f32[32,128]{1,0:T(8,128)S(1)} %get-tuple-element.41), channel_id=1, source_target_pairs={{0,4},{1,5},{2,6},{3,7},{4,0},{5,1},{6,2},{7,3},{8,12},{9,13},{10,... | collective-permute-start | bytes 49160 | tf_op jit(solution)/shard_map/ppermute | solution.py:373
  20.1 4.1 %collective-permute-start.6 = (f32[32,128]{1,0:T(8,128)S(1)}, f32[32,128]{1,0:T(8,128)S(1)}, u32[]{:S(2)}, u32[]{:S(2)}) collective-permute-start(f32[32,128]{1,0:T(8,128)S(1)} %get-tuple-element.42), channel_id=1, source_target_pairs={{0,28},{1,29},{2,30},{3,31},{4,8},{5,9},{6,10},{7,11},{8,4},{9,5},... | collective-permute-start | bytes 49160 | tf_op jit(solution)/shard_map/ppermute | solution.py:372

commit v3 on v2

v3 whole, which is shorter than its diff:
```python
import functools

import jax
import jax.numpy as jnp
from jax import lax
from jax.experimental import pallas as pl
from jax.experimental.pallas import tpu as pltpu
from jax.sharding import PartitionSpec as P

BLOCK = 8
NC = 16
LANES = 128
ROWS = 32
NEAR = 128
FAR = 32
VMEM_BYTES = 12 * 2**20
damping = 0.8

f32 = jnp.float32
bf16 = jnp.bfloat16


def roll(value, shift, axis):
    return pltpu.roll(value, shift % value.shape[axis], axis)


def around(value, step):
    rows = roll(value, 1, 0) + roll(value, -1, 0)
    return rows + (roll(value, step, 1) + roll(value, -step, 1))


def iota(shape, axis):
    return lax.broadcasted_iota(jnp.int32, shape, axis)


def ones_where(condition):
    return jnp.where(condition, 1.0, 0.0).astype(f32)


def pack_near_far(tiles, near_tile, far_tile, far_lane):
    far = tiles[:, far_tile * LANES : (far_tile + 1) * LANES]
    near = tiles[:, near_tile * LANES : (near_tile + 1) * LANES]
    count = LANES // FAR
    group = tiles.shape[0] // count
    lane = iota((group, LANES), 1) // FAR
    packed = jnp.zeros((group, LANES), f32)
    for g in range(count):
        moved = roll(far[g * group : (g + 1) * group], FAR * g - far_lane, 1)
        packed = jnp.where(lane == g, moved, packed)
    return near, packed


def edges_kernel(*refs):
    ins, right_ref, reaction_ref, even_ref, odd_ref, rows_ref = refs[:3], *refs[3:8]
    kappa_ref, ice_ref, sems = refs[8:11]
    copies = []
    for k, (src, dst) in enumerate(zip(ins, (right_ref, kappa_ref, ice_ref))):
        copies.append(pltpu.make_async_copy(src, dst, sems.at[k]))
    for copy in copies:
        copy.start()
    height, width = right_ref.shape
    blocks = ice_ref.shape
    spread = ones_where(iota((blocks[1], width), 1) // BLOCK == iota((blocks[1], width), 0))
    repeat = ones_where(iota((height, blocks[0]), 0) // BLOCK == iota((height, blocks[0]), 1))
    for copy in copies:
        copy.wait()
    ice = ice_ref[...].astype(f32)
    ice = jnp.dot(ice, spread, preferred_element_type=f32)
    ice = jnp.dot(repeat, ice, preferred_element_type=f32)
    reaction = kappa_ref[...] * (1.0 + 3.0 * (1.0 - ice))
    reaction_ref[...] = reaction
    tiles = width // LANES
    even = lax.rem(lax.axis_index("gy"), 2) == 0
    even_row = lax.rem(lax.axis_index("gx"), 2) == 0
    size = height + height * FAR // LANES
    for k, field in enumerate((right_ref[...], reaction)):
        to_right = pack_near_far(field, tiles - 1, tiles - 2, LANES - FAR)
        to_left = pack_near_far(field, 0, 1, 0)
        start = k * size
        for a, b in zip(to_right, to_left):
            stop = start + a.shape[0]
            even_ref[start:stop, :] = jnp.where(even, a, b)
            odd_ref[start:stop, :] = jnp.where(even, b, a)
            start = stop
        edge = jnp.where(even_row, field[:ROWS], field[height - ROWS :])
        for j in range(tiles):
            rows_ref[k * tiles + j] = edge[:, j * LANES : (j + 1) * LANES]


def exact_dot(value, table):
    rows = value.shape[0]
    parts = []
    for _ in range(3):
        part = value.astype(bf16)
        parts.append(part)
        value = value - part.astype(f32)
    out = jnp.dot(jnp.concatenate(parts, axis=0), table.astype(bf16), preferred_element_type=f32)
    return out[:rows] + out[rows : 2 * rows] + out[2 * rows :]


def own_tile(own_ref, even_ref, odd_ref, even, k, j, start, count):
    height, width = own_ref.shape
    tiles = width // LANES
    size = even_ref.shape[0] // 2
    if 1 <= j <= tiles:
        return own_ref[start : start + count, (j - 1) * LANES : j * LANES]
    if j <= tiles + 1:
        rows = pl.ds(k * size + start, count)
        first, second = even_ref[rows, :], odd_ref[rows, :]
        return jnp.where(even, first, second) if j else jnp.where(even, second, first)
    group = height * FAR // LANES
    g = start // group
    rows = pl.ds(k * size + height + start % group, count)
    first, second = even_ref[rows, :], odd_ref[rows, :]
    lane = iota((count, LANES), 1)
    right = roll(jnp.where(even, first, second), -FAR * g, 1)
    left = roll(jnp.where(even, second, first), LANES - FAR - FAR * g, 1)
    return jnp.where(lane < FAR, right, jnp.where(lane >= LANES - FAR, left, 0.0))


def rows_kernel(right_ref, reaction_ref, even_ref, odd_ref, unread_ref, even_out, odd_out):
    height, width = right_ref.shape
    tiles = width // LANES
    even_column = lax.rem(lax.axis_index("gy"), 2) == 0
    even_row = lax.rem(lax.axis_index("gx"), 2) == 0
    far = []
    for k, ref in enumerate((right_ref, reaction_ref)):
        for j in range(tiles + 3):
            up = own_tile(ref, even_ref, odd_ref, even_column, k, j, 0, ROWS)
            down = own_tile(ref, even_ref, odd_ref, even_column, k, j, height - ROWS, ROWS)
            even_out[k * (tiles + 3) + j] = jnp.where(even_row, down, up)
            odd = jnp.where(even_row, up, down)
            if j in (0, tiles + 1):
                odd_out[2 * k + (j > 0)] = odd
            elif j > tiles:
                far.append(odd)
    lane = iota((ROWS, LANES), 1)
    odd_out[4] = jnp.where((lane >= FAR) & (lane < LANES - FAR), roll(far[1], LANES // 2, 1), far[0])


def beside(tiles, step):
    lane = iota(tiles[0].shape, 1)
    forward = [roll(t, step, 1) for t in tiles]
    backward = [roll(t, -step, 1) for t in tiles]
    count = len(tiles)
    return [
        jnp.where(lane < step, forward[j - 1], forward[j])
        + jnp.where(lane >= LANES - step, backward[(j + 1) % count], backward[j])
        for j in range(count)
    ]


def around_strip(ref, row, step):
    count = ref.shape[0]
    here = [ref[j, row : row + 8] for j in range(count)]
    side = beside(here, step)
    total = [(ref[j, row - 1 : row + 7] + ref[j, row + 1 : row + 9]) + side[j] for j in range(count)]
    return here, total


def down_kernel(counts, *refs):
    right_ref, reaction_ref, even_ref, odd_ref, even_rows, odd_rows, odd_corners = refs[:7]
    starts, fields, gains = refs[7:10], refs[10:13], refs[13:16]
    own_out, even_out, odd_out = refs[16:19]
    sources, reactions, residuals = refs[19:22], refs[22:25], refs[25:28]
    height, width = right_ref.shape
    tiles = width // LANES
    count = tiles + 3
    gx, gy = lax.axis_index("gx"), lax.axis_index("gy")
    even_column = lax.rem(gy, 2) == 0
    even_row = lax.rem(gx, 2) == 0
    zero = jnp.zeros((8, LANES), f32)
    lane = iota((8, LANES), 1)
    top_in = jnp.where(gx > 0, 1.0, 0.0).astype(f32)
    bottom_in = jnp.where(gx < counts[0] - 1, 1.0, 0.0).astype(f32)
    left_in = jnp.where(gy > 0, damping, 0.0).astype(f32)
    right_in = jnp.where(gy < counts[1] - 1, damping, 0.0).astype(f32)
    scale = [jnp.full((8, LANES), damping, f32)] * count
    scale[0] = jnp.full((8, LANES), left_in, f32)
    scale[tiles + 1] = jnp.full((8, LANES), right_in, f32)
    scale[tiles + 2] = jnp.where(lane < FAR, right_in, jnp.where(lane >= LANES - FAR, left_in, 0.0))

    def first_tile(k, j, row):
        own = (right_ref, reaction_ref)[k]
        if ROWS <= row < ROWS + height:
            return own_tile(own, even_ref, odd_ref, even_column, k, j, row - ROWS, 8)
        top = row < ROWS
        row = row if top else row - ROWS - height
        if 1 <= j <= tiles:
            odd = odd_rows[k * tiles + j - 1, row : row + 8]
        elif j <= tiles + 1:
            odd = odd_corners[2 * k + (j > 0), row : row + 8]
        else:
            odd = odd_corners[4, row : row + 8]
            odd = roll(odd, LANES // 2, 1) if k else odd
        even = even_rows[k * count + j, row : row + 8]
        return jnp.where(even_row, odd, even) if top else jnp.where(even_row, even, odd)

    def paired(ref, row, step, lanes=True):
        pairs = [
            ref[j, pl.ds(2 * row + 8, 8, stride=2), :] + ref[j, pl.ds(2 * row + 9, 8, stride=2), :]
            for j in range(count)
        ]
        if not lanes:
            return pairs
        moved = [roll(t, -step, 1) for t in pairs]
        return [
            0.25 * (pairs[j] + jnp.where(lane >= LANES - step, moved[(j + 1) % count], moved[j]))
            for j in range(count)
        ]

    margin = ROWS
    for level in range(3):
        rows = (height >> level) + 2 * margin
        stiffness = 0.25**level
        step = 2**level
        start, field, gain = starts[level], fields[level], gains[level]
        source, reaction, residual = sources[level], reactions[level], residuals[level]
        for ref in (start, field):
            for j in range(count):
                ref[j, :8] = zero
                ref[j, rows + 8 :] = zero
        for row in range(0, rows, 8):
            if level == 0:
                pieces = [[first_tile(k, j, row) for j in range(count)] for k in range(2)]
            else:
                pieces = [
                    paired(ref[level - 1], row, step // 2) for ref in (residuals, reactions)
                ]
            for j in range(count):
                value = scale[j] / (pieces[1][j] + 4.0 * stiffness)
                if row < margin:
                    value = value * top_in
                elif row >= rows - margin:
                    value = value * bottom_in
                place = pl.ds(row + 8, 8)
                source[j, place] = pieces[0][j]
                reaction[j, place] = pieces[1][j]
                start[j, place] = value * pieces[0][j]
                gain[j, place] = value * stiffness if level else value
        for row in range(8, rows + 8, 8):
            here, total = around_strip(start, row, step)
            for j in range(count):
                field[j, row : row + 8] = (2.0 - damping) * here[j] + gain[j, row : row + 8] * total[j]
        for row in range(8, rows + 8, 8):
            here, total = around_strip(field, row, step)
            for j in range(count):
                place = pl.ds(row, 8)
                diagonal = reaction[j, place] + 4.0 * stiffness
                near = stiffness * total[j] if level else total[j]
                residual[j, place] = (source[j, place] - diagonal * here[j]) + near
        margin //= 2
    total = count * LANES
    cell = iota((total, LANES), 0)
    step = 4
    target = jnp.where(cell >= total - FAR, cell - total + 8 * LANES, cell) // 8
    valid = (cell % step == 0) & ((cell < total - LANES + FAR) | (cell >= total - FAR))
    gather = ones_where(valid & (target == iota((total, LANES), 1)))
    coarse_rows = height // 8 + 2 * margin
    strips = []
    for ref in (residuals[2], reactions[2]):
        for row in range(0, coarse_rows, 8):
            strips.append(jnp.concatenate(paired(ref, row, step, lanes=False), axis=1))
    compact = 0.25 * exact_dot(jnp.concatenate(strips, axis=0), gather)
    own_out[...] = compact
    half = height // 8
    for k in range(2):
        base = k * coarse_rows + margin
        to_next = compact[base - 1 : base - 1 + half]
        to_last = compact[base + 1 : base + 1 + half]
        even_out[k * half : (k + 1) * half] = jnp.where(even_row, to_next, to_last)
        odd_out[k * half : (k + 1) * half] = jnp.where(even_row, to_last, to_next)


def up_kernel(counts, *refs):
    starts, befores, gains = refs[:3], refs[3:6], refs[6:9]
    own_ref, even_ref, odd_ref = refs[9:12]
    out_ref = refs[12]
    region = refs[13]
    firsts, seconds = refs[14:17], refs[17:20]
    buffer, sems = refs[20:22]
    height, width = out_ref.shape
    tiles = width // LANES
    gx, gy = lax.axis_index("gx"), lax.axis_index("gy")
    even_row = lax.rem(gx, 2) == 0
    half = height // 8
    coarse_rows = own_ref.shape[0] // 2
    margin = (coarse_rows - half) // 2
    lead = 8 + half
    rows = region.shape[1]
    region[...] = jnp.zeros_like(region)
    for k in range(2):
        a = even_ref[k * half : (k + 1) * half]
        b = odd_ref[k * half : (k + 1) * half]
        own = own_ref[k * coarse_rows : (k + 1) * coarse_rows]
        region[k, lead - 1 - half : lead - 1] = jnp.where(even_row, b, a)
        region[k, lead - 1 : lead + half + 1] = own[margin - 1 : margin + half + 1]
        region[k, lead + half + 1 : lead + 2 * half + 1] = jnp.where(even_row, a, b)
    stiffness = 0.25**3
    row = gx * half - lead + iota((rows, LANES), 0)
    col = iota((rows, LANES), 1)
    col = jnp.where(col >= LANES - FAR // 8, col - LANES, col) - NEAR // 8
    col = col + gy * (width // 8)
    inside = (row >= 0) & (row < counts[0] * half) & (col >= 0) & (col < counts[1] * (width // 8))
    gain = ones_where(inside) * (damping / (region[1] + 4.0 * stiffness))
    field = gain * region[0]
    constant = field
    gain = gain * stiffness
    for sweep in range(NC - 1):
        field = (1.0 - damping) * field + constant + gain * around(field, 1)
    field = field[lead - margin : lead - margin + coarse_rows]
    total = width + LANES
    position = iota((LANES, total), 1)
    position = jnp.where(position >= width + LANES // 2, position - total, position)
    expand = ones_where((position + NEAR) // 8 == iota((LANES, total), 0))
    field = exact_dot(field, expand)
    lane = iota((8, LANES), 1)
    zero = jnp.zeros((8, LANES), f32)

    def tile_of(ref, j, place):
        if j < tiles:
            return ref[j + 1, place, :]
        return jnp.where(lane < LANES // 2, ref[tiles + 1, place, :], ref[0, place, :])

    def begin(level, row, pieces):
        shift = (befores[level].shape[1] - firsts[level].shape[1]) // 2
        for j, piece in enumerate(pieces):
            for odd in range(2):
                place = pl.ds(2 * row + 8 - shift + odd, 8, stride=2)
                from_place = pl.ds(2 * row + 8 + odd, 8, stride=2)
                firsts[level][j, place, :] = tile_of(befores[level], j, from_place) + piece

    def sweep_strip(ref, level, row, count):
        base = (starts[level].shape[1] - ref.shape[1]) // 2
        here, total = around_strip(ref, row, 2**level)
        place = pl.ds(row + base, 8)
        return [
            ((1.0 - damping) * here[j] + tile_of(starts[level], j, place))
            + tile_of(gains[level], j, place) * total[j]
            for j in range(count)
        ]

    for row in range(0, coarse_rows, 8):
        begin(2, row, [field[row : row + 8, j * LANES : (j + 1) * LANES] for j in range(tiles + 1)])
    for level in (2, 1, 0):
        first, second = firsts[level], seconds[level]
        rows = first.shape[1] - 16
        step = 2**level
        skip = 8 if level < 2 else 0
        for j in range(tiles + 1):
            for ref in (first, second) if level == 2 else (second,):
                ref[j, skip : skip + 8] = zero
                ref[j, rows + 8 - skip : rows + 16 - skip] = zero
        for row in range(8 + skip, rows + 8 - skip, 8):
            pieces = sweep_strip(first, level, row, tiles + 1)
            for j in range(tiles + 1):
                second[j, row : row + 8] = pieces[j]
        if level > 0:
            bit = step // 2
            for row in range(8 + skip, rows + 8 - skip, 8):
                pieces = sweep_strip(second, level, row, tiles + 1)
                moved = [roll(t, bit, 1) for t in pieces]
                pieces = [
                    jnp.where(
                        (lane // bit) % 2 == 1,
                        jnp.where(lane < bit, moved[j - 1], moved[j]),
                        pieces[j],
                    )
                    for j in range(tiles + 1)
                ]
                begin(level - 1, row - 8, pieces)
        else:
            chunk = height // sems.shape[0]
            copies = []
            for row in range(0, height, 8):
                pieces = sweep_strip(second, level, row + 8 + (rows - height) // 2, tiles)
                for j in range(tiles):
                    buffer[row : row + 8, j * LANES : (j + 1) * LANES] = pieces[j]
                if (row + 8) % chunk == 0:
                    place = pl.ds(row + 8 - chunk, chunk)
                    copy = pltpu.make_async_copy(buffer.at[place], out_ref.at[place], sems.at[row // chunk])
                    copy.start()
                    copies.append(copy)
            for copy in copies:
                copy.wait()


def swap_pairs(counts, axis):
    nx, ny = counts
    even, odd = [], []
    for i in range(nx):
        for j in range(ny):
            here = i * ny + j
            place = (i, j)[axis]
            last = counts[axis] - 1
            hop = ny if axis == 0 else 1
            even.append((here, here + hop * (1 - 2 * (place % 2))))
            if place in (0, last):
                other = ((last - i) * ny + j) if axis == 0 else ((i ^ 1) * ny + j)
                odd.append((here, other))
            else:
                odd.append((here, here + hop * (2 * (place % 2) - 1)))
    return even, odd


def params():
    return pltpu.CompilerParams(vmem_limit_bytes=VMEM_BYTES)


def shape(*dims):
    return jax.ShapeDtypeStruct(dims, f32)


def per_device(counts, right_side, kappa_field, ice_blocks):
    height, width = right_side.shape
    tiles = width // LANES
    count = tiles + 3
    axes = ("gx", "gy")
    right_side, kappa_field, ice_blocks = [
        pltpu.with_memory_space_constraint(x, pltpu.HBM) for x in (right_side, kappa_field, ice_blocks)
    ]
    row_even, row_odd = swap_pairs(counts, 0)
    col_even, col_odd = swap_pairs(counts, 1)
    packed = 2 * (height + height * FAR // LANES)
    right_side, reaction, even, odd, odd_rows = pl.pallas_call(
        edges_kernel,
        out_shape=(
            shape(height, width),
            shape(height, width),
            shape(packed, LANES),
            shape(packed, LANES),
            shape(2 * tiles, ROWS, LANES),
        ),
        in_specs=[pl.BlockSpec(memory_space=pltpu.HBM)] * 3,
        scratch_shapes=[
            pltpu.VMEM((height, width), f32),
            pltpu.VMEM(ice_blocks.shape, jnp.int32),
            pltpu.SemaphoreType.DMA((3,)),
        ],
        compiler_params=params(),
        name="edges",
    )(right_side, kappa_field, ice_blocks)
    odd_rows = lax.ppermute(odd_rows, axes, row_odd)
    odd = lax.ppermute(odd, axes, col_odd)
    even = lax.ppermute(even, axes, col_even)
    even_rows, odd_corners = pl.pallas_call(
        rows_kernel,
        out_shape=(shape(2 * count, ROWS, LANES), shape(5, ROWS, LANES)),
        compiler_params=params(),
        name="rows",
    )(right_side, reaction, even, odd, odd_rows)
    odd_corners = lax.ppermute(odd_corners, axes, row_odd)
    even_rows = lax.ppermute(even_rows, axes, row_even)
    half = height // 8
    levels = [(count, ((height + 2 * ROWS) >> level) + 16, LANES) for level in range(3)]
    coarse_rows = half + ROWS // 4
    outs = pl.pallas_call(
        functools.partial(down_kernel, counts),
        out_shape=(
            *[shape(*dims) for dims in levels * 3],
            shape(2 * coarse_rows, LANES),
            shape(2 * half, LANES),
            shape(2 * half, LANES),
        ),
        scratch_shapes=[pltpu.VMEM(dims, f32) for dims in levels * 3],
        compiler_params=params(),
        name="down",
    )(right_side, reaction, even, odd, even_rows, odd_rows, odd_corners)
    posts, own, even, odd = outs[:9], outs[9], outs[10], outs[11]
    odd = lax.ppermute(odd, axes, row_odd)
    even = lax.ppermute(even, axes, row_even)
    fields = [(tiles + 1, (height >> level) + 2 * (16 if level < 2 else 8) + 16, LANES) for level in range(3)]
    return pl.pallas_call(
        functools.partial(up_kernel, counts),
        out_shape=shape(height, width),
        out_specs=pl.BlockSpec(memory_space=pltpu.HBM),
        scratch_shapes=[
            pltpu.VMEM((2, half * 3 + 16, LANES), f32),
            *[pltpu.VMEM(dims, f32) for dims in fields * 2],
            pltpu.VMEM((height, width), f32),
            pltpu.SemaphoreType.DMA((4,)),
        ],
        compiler_params=params(),
        name="up",
    )(*posts, own, even, odd)


def solution(mesh):
    counts = (mesh.shape["gx"], mesh.shape["gy"])
    return jax.shard_map(
        functools.partial(per_device, counts),
        mesh=mesh,
        in_specs=(P("gx", "gy"),) * 3,
        out_specs=P("gx", "gy"),
        check_vma=False,
    )
```

time: 27.5 us -> 26.5 us (0.964)
  Pallas kernels: 7.73 us -> 6.71 us
    pallas_call x3, Pallas kernels: 6.31 us -> 5.3 us  [the longest x1 3.11 us: per_device(): pl.pallas_call(functools.partial(up_kernel, counts), out_shape=shape(heig...]
where the time goes in v3:
time: 26.5 us; the launch traced here: 26.4 us
  waiting for transfers between devices  13.4 us (51%)
  Pallas kernels  6.71 us (25%)
  starting transfers between devices  6.19 us (23%)
    ppermute x1, waiting for transfers between devices, per_device(): odd_rows = lax.ppermute(odd_rows, axes, row_odd)  5.27 us
    ppermute x1, waiting for transfers between devices, per_device(): odd_corners = lax.ppermute(odd_corners, axes, row_odd)  4.42 us
    ppermute x1, starting transfers between devices, per_device(): odd = lax.ppermute(odd, axes, col_odd)  3.14 us
    pallas_call x1, Pallas kernels, per_device(): pl.pallas_call(functools.partial(up_kernel, counts), out_shape=shape(heig...  3.11 us
    ppermute x1, waiting for transfers between devices, per_device(): odd = lax.ppermute(odd, axes, row_odd)  2.96 us
    pallas_call x1, Pallas kernels, per_device(): pl.pallas_call(functools.partial(down_kernel, counts), out_shape=(*[shape...  2.03 us
    pallas_call x1, Pallas kernels, per_device(): pl.pallas_call(edges_kernel, out_shape=(shape(height, width), shape(heigh...  1.42 us
    ppermute x1, starting transfers between devices, per_device(): odd_rows = lax.ppermute(odd_rows, axes, row_odd)  1.33 us
  transfers between devices with their start and end apart: 7, of which 4 were waited for; matrix products, arithmetic and copies ran while one was open for 0% of the time, Pallas kernels for 0%

profile of v3, /device:TPU:8, one launch (start us, length us, event | category | flops | bytes accessed | tf_op | source)
XLA Modules:
  0.0 26.4 jit_solution(1160414083759295864)
XLA Ops:
  0.0 1.4 %edges.1 = (f32[128,512]{1,0:T(8,128)S(1)}, f32[128,512]{1,0:T(8,128)S(1)}, f32[320,128]{1,0:T(8,128)S(1)}, f32[320,128]{1,0:T(8,128)S(1)}, f32[8,32,128]{2,1,0:T(8,128)S(1)}) custom-call(f32[128,512]{1,0:T(8,128)} %refs_0_.1, f32[128,512]{1,0:T(8,128)} %refs_1_.1, s32[16,64]{1,0:T(8,128)} %refs_2_.1), custom_call_target="tpu_custom_call" | custom-call | tf_op jit(solution)/shard_map/edges/pallas_call | solution.py:425
  1.4 0.1 collective-permute-start
  1.5 3.1 %collective-permute-start.1 = (f32[320,128]{1,0:T(8,128)S(1)}, f32[320,128]{1,0:T(8,128)S(1)}, u32[]{:S(2)}, u32[]{:S(2)}) collective-permute-start(f32[320,128]{1,0:T(8,128)S(1)} %get-tuple-element.27), channel_id=1, source_target_pairs={{0,4},{1,2},{2,1},{3,7},{4,0},{5,6},{6,5},{7,3},{8,12},{9,10},{10,... | collective-permute-start | bytes 491528 | tf_op jit(solution)/shard_map/ppermute | solution.py:444
  4.6 1.3 %collective-permute-start.2 = (f32[8,32,128]{2,1,0:T(8,128)S(1)}, f32[8,32,128]{2,1,0:T(8,128)S(1)}, u32[]{:S(2)}, u32[]{:S(2)}) collective-permute-start(f32[8,32,128]{2,1,0:T(8,128)S(1)} %get-tuple-element.28), channel_id=1, source_target_pairs={{0,28},{1,29},{2,30},{3,31},{4,8},{5,9},{6,10},{7,11},{8,4},{9,5},... | collective-permute-start | bytes 393224 | tf_op jit(solution)/shard_map/ppermute | solution.py:443
  6.0 5.3 %collective-permute-done.2.unread_ref.refs_5_ = f32[8,32,128]{2,1,0:T(8,128)S(1)} collective-permute-done((f32[8,32,128]{2,1,0:T(8,128)S(1)}, f32[8,32,128]{2,1,0:T(8,128)S(1)}, u32[]{:S(2)}, u32[]{:S(2)}) %collective-permute-start.2) | collective-permute-done | bytes 131104 | tf_op jit(solution)/shard_map/ppermute | solution.py:443
  11.2 0.0 collective-permute-done.even_ref.refs_2_
  11.2 0.0 collective-permute-done.1.odd_ref.refs_3_
  11.2 0.2 rows.1
  11.4 0.0 collective-permute-start.3
  11.4 1.2 %collective-permute-start.4 = (f32[5,32,128]{2,1,0:T(8,128)S(1)}, f32[5,32,128]{2,1,0:T(8,128)S(1)}, u32[]{:S(2)}, u32[]{:S(2)}) collective-permute-start(f32[5,32,128]{2,1,0:T(8,128)S(1)} %get-tuple-element.30), channel_id=1, source_target_pairs={{0,28},{1,29},{2,30},{3,31},{4,8},{5,9},{6,10},{7,11},{8,4},{9,5},... | collective-permute-start | bytes 245768 | tf_op jit(solution)/shard_map/ppermute | solution.py:452
  12.6 4.4 %collective-permute-done.4.refs_6_ = f32[5,32,128]{2,1,0:T(8,128)S(1)} collective-permute-done((f32[5,32,128]{2,1,0:T(8,128)S(1)}, f32[5,32,128]{2,1,0:T(8,128)S(1)}, u32[]{:S(2)}, u32[]{:S(2)}) %collective-permute-start.4) | collective-permute-done | bytes 81952 | tf_op jit(solution)/shard_map/ppermute | solution.py:452
  17.0 0.0 collective-permute-done.3.refs_4_
  17.0 2.0 %down.1 = (f32[7,208,128]{2,1,0:T(8,128)S(1)}, f32[7,112,128]{2,1,0:T(8,128)S(1)}, f32[7,64,128]{2,1,0:T(8,128)S(1)}, f32[7,208,128]{2,1,0:T(8,128)S(1)}, f32[7,...) custom-call(f32[128,512]{1,0:T(8,128)S(1)} %get-tuple-element.24.rig, ...), custom_call_target="tpu_custom_call" | custom-call | tf_op jit(solution)/shard_map/down/pallas_call | solution.py:457
  19.0 0.1 collective-permute-start.5
  19.1 0.4 %collective-permute-start.6 = (f32[32,128]{1,0:T(8,128)S(1)}, f32[32,128]{1,0:T(8,128)S(1)}, u32[]{:S(2)}, u32[]{:S(2)}) collective-permute-start(f32[32,128]{1,0:T(8,128)S(1)} %get-tuple-element.42), channel_id=1, source_target_pairs={{0,28},{1,29},{2,30},{3,31},{4,8},{5,9},{6,10},{7,11},{8,4},{9,5},... | collective-permute-start | bytes 49160 | tf_op jit(solution)/shard_map/ppermute | solution.py:470
  19.5 0.8 %collective-permute-done.5.refs_10_ = f32[32,128]{1,0:T(8,128)S(1)} collective-permute-done((f32[32,128]{1,0:T(8,128)S(1)}, f32[32,128]{1,0:T(8,128)S(1)}, u32[]{:S(2)}, u32[]{:S(2)}) %collective-permute-start.5) | collective-permute-done | bytes 16416 | tf_op jit(solution)/shard_map/ppermute | solution.py:471
  20.3 3.0 %collective-permute-done.6.refs_11_ = f32[32,128]{1,0:T(8,128)S(1)} collective-permute-done((f32[32,128]{1,0:T(8,128)S(1)}, f32[32,128]{1,0:T(8,128)S(1)}, u32[]{:S(2)}, u32[]{:S(2)}) %collective-permute-start.6) | collective-permute-done | bytes 16416 | tf_op jit(solution)/shard_map/ppermute | solution.py:470
  23.2 3.1 %up.1 = f32[128,512]{1,0:T(8,128)} custom-call(f32[7,208,128]{2,1,0:T(8,128)S(1)} %get-tuple-element.31.refs_0_, f32[7,112,128]{2,1,0:T(8,128)S(1)} %get-tuple-element.32.refs_1_, f32[7,64,128]{2,1,0:T(8,128)S(1)} %get-tuple-element.33.refs_2_, f32[7,208,128]{2,1,0:T(8,128)S(1)} %get-tuple-element.34.refs_3_, f32[7,112,128]{2,1,0:T(8,128)S(1)} %get-tuple-element.35.refs_4_, ...), custom_call_target="tpu_custom_call" | custom-call | tf_op jit(solution)/shard_map/up/pallas_call | solution.py:473
Async XLA Ops:
  1.4 9.8 %collective-permute-start = (f32[320,128]{1,0:T(8,128)S(1)}, f32[320,128]{1,0:T(8,128)S(1)}, u32[]{:S(2)}, u32[]{:S(2)}) collective-permute-start(f32[320,128]{1,0:T(8,128)S(1)} %get-tuple-element.26), channel_id=1, source_target_pairs={{0,1},{1,0},{2,3},{3,2},{4,5},{5,4},{6,7},{7,6},{8,9},{9,8},{10,11... | collective-permute-start | bytes 491528 | tf_op jit(solution)/shard_map/ppermute | solution.py:445
  1.5 9.7 %collective-permute-start.1 = (f32[320,128]{1,0:T(8,128)S(1)}, f32[320,128]{1,0:T(8,128)S(1)}, u32[]{:S(2)}, u32[]{:S(2)}) collective-permute-start(f32[320,128]{1,0:T(8,128)S(1)} %get-tuple-element.27), channel_id=1, source_target_pairs={{0,4},{1,2},{2,1},{3,7},{4,0},{5,6},{6,5},{7,3},{8,12},{9,10},{10,... | collective-permute-start | bytes 491528 | tf_op jit(solution)/shard_map/ppermute | solution.py:444
  4.6 6.6 %collective-permute-start.2 = (f32[8,32,128]{2,1,0:T(8,128)S(1)}, f32[8,32,128]{2,1,0:T(8,128)S(1)}, u32[]{:S(2)}, u32[]{:S(2)}) collective-permute-start(f32[8,32,128]{2,1,0:T(8,128)S(1)} %get-tuple-element.28), channel_id=1, source_target_pairs={{0,28},{1,29},{2,30},{3,31},{4,8},{5,9},{6,10},{7,11},{8,4},{9,5},... | collective-permute-start | bytes 393224 | tf_op jit(solution)/shard_map/ppermute | solution.py:443
  11.4 5.6 %collective-permute-start.3 = (f32[14,32,128]{2,1,0:T(8,128)S(1)}, f32[14,32,128]{2,1,0:T(8,128)S(1)}, u32[]{:S(2)}, u32[]{:S(2)}) collective-permute-start(f32[14,32,128]{2,1,0:T(8,128)S(1)} %get-tuple-element.29), channel_id=1, source_target_pairs={{0,4},{1,5},{2,6},{3,7},{4,0},{5,1},{6,2},{7,3},{8,12},{9,13},{10,... | collective-permute-start | bytes 688136 | tf_op jit(solution)/shard_map/ppermute | solution.py:453
  11.4 5.6 %collective-permute-start.4 = (f32[5,32,128]{2,1,0:T(8,128)S(1)}, f32[5,32,128]{2,1,0:T(8,128)S(1)}, u32[]{:S(2)}, u32[]{:S(2)}) collective-permute-start(f32[5,32,128]{2,1,0:T(8,128)S(1)} %get-tuple-element.30), channel_id=1, source_target_pairs={{0,28},{1,29},{2,30},{3,31},{4,8},{5,9},{6,10},{7,11},{8,4},{9,5},... | collective-permute-start | bytes 245768 | tf_op jit(solution)/shard_map/ppermute | solution.py:452
  19.0 1.2 %collective-permute-start.5 = (f32[32,128]{1,0:T(8,128)S(1)}, f32[32,128]{1,0:T(8,128)S(1)}, u32[]{:S(2)}, u32[]{:S(2)}) collective-permute-start(f32[32,128]{1,0:T(8,128)S(1)} %get-tuple-element.41), channel_id=1, source_target_pairs={{0,4},{1,5},{2,6},{3,7},{4,0},{5,1},{6,2},{7,3},{8,12},{9,13},{10,... | collective-permute-start | bytes 49160 | tf_op jit(solution)/shard_map/ppermute | solution.py:471
  19.1 4.1 %collective-permute-start.6 = (f32[32,128]{1,0:T(8,128)S(1)}, f32[32,128]{1,0:T(8,128)S(1)}, u32[]{:S(2)}, u32[]{:S(2)}) collective-permute-start(f32[32,128]{1,0:T(8,128)S(1)} %get-tuple-element.42), channel_id=1, source_target_pairs={{0,28},{1,29},{2,30},{3,31},{4,8},{5,9},{6,10},{7,11},{8,4},{9,5},... | collective-permute-start | bytes 49160 | tf_op jit(solution)/shard_map/ppermute | solution.py:470
